TPU v7x, 32 devices: a whole 2x2x4 slice. The times are simulated.
32 devices in a mesh: gx: 4 (over y, x), gy: 4 (over z), gz: 2 (over core).
Axes of the slice: x: 2, y: 2, z: 4, core: 2. Of those that a mesh axis runs over, the one named last changes fastest.
Arguments:
- positions: float32 [12, 12, 16, 96], P('gx', 'gy', 'gz'), may hold values from 0 to 1
- types: int32 [12, 12, 16, 32], P('gx', 'gy', 'gz'), may hold values from 0 to 2
Outputs:
- forces_energy: float32 [12, 12, 16, 128], P('gx', 'gy', 'gz')
Inputs may be any that keep to these rules, and one draw needn't show every extreme that they name: `types`: 0 marks an empty slot, 1 a copper atom, 2 a nickel atom.
All inputs are finite; a program needn't handle non-finite values.
Results may differ from a plain program's by a relative error of at most 0.0001.
Values sent between devices are 32-bit elements; how exact they have to be, the bound alone decides.
No kernel may reach another device: no remote copies, remote signals or barrier semaphores. Data moves between devices by JAX's collectives and lax.ppermute only.
A program may use at most 64 MiB of HBM per device.

v0:
```python
import jax
import jax.numpy as jnp
from jax import lax
from jax.sharding import PartitionSpec as P

cut_square = 0.9025
density_rate = 3.0
pair_rate = 6.0


def padded_2(value, sides, width):
    for axis, dim in sides:
        peers, length = (lax.axis_size(axis), value.shape[dim])
        up = [(i, (i + 1) % peers) for i in range(peers)]
        down = [(j, i) for i, j in up]
        last = lax.slice_in_dim(value, length - width, length, axis=dim)
        first = lax.slice_in_dim(value, 0, width, axis=dim)
        before = lax.ppermute(last, axis, up)
        after = lax.ppermute(first, axis, down)
        value = jnp.concatenate([before, value, after], axis=dim)
    return value


def type_tables(types):
    weight = jnp.where(types == 1, 1.0, jnp.where(types == 2, 1.6, 0.0)).astype(jnp.float32)
    embedding = jnp.where(types == 1, 1.0, jnp.where(types == 2, 1.4, 0.0)).astype(jnp.float32)
    return (weight, embedding)


def separation(own_coords, other_coords, cell_shift):
    shift_vector = jnp.asarray(cell_shift, jnp.float32).reshape(3, 1, 1)
    displace = shift_vector + other_coords[..., :, None, :] - own_coords[..., :, :, None]
    return (displace, jnp.sum(displace * displace, axis=-3))


def density_shape(square):
    margin = jnp.maximum(1.0 - square / cut_square, 0.0)
    return jnp.exp(-density_rate * square) * margin * margin


def all_shapes(square):
    margin = jnp.maximum(1.0 - square / cut_square, 0.0)
    density_exponent = jnp.exp(-density_rate * square)
    pair_exp = jnp.exp(-pair_rate * square)
    dens_slope = -density_exponent * margin * (density_rate * margin + 2.0 / cut_square)
    pair_value = pair_exp * margin * margin
    pair_slope = -pair_exp * margin * (pair_rate * margin + 2.0 / cut_square)
    return (dens_slope, pair_value, pair_slope)


def half_shifts():
    upward = [
        (a, b, c) for a in (-1, 0, 1) for b in (-1, 0, 1) for c in (-1, 0, 1) if a + b + c > 0
    ]
    return [(0, 0, 0)] + upward + [(1, -1, 0), (0, 1, -1), (-1, 0, 1)]


def fold_classes():
    return [(0,), (1,), (2,), (0, 1), (0, 2), (1, 2), (0, 1, 2)]


def class_fold(block, members):
    for axis_index in range(3):
        inner = block.shape[axis_index] - 2
        if axis_index in members:
            lower = lax.slice_in_dim(block, 0, 1, axis=axis_index)
            upper = lax.slice_in_dim(block, inner + 1, inner + 2, axis=axis_index)
            middle_shape = list(block.shape)
            middle_shape[axis_index] = inner - 2
            middle = jnp.zeros(tuple(middle_shape), block.dtype)
            block = jnp.concatenate([lower, middle, upper], axis=axis_index)
        else:
            block = lax.slice_in_dim(block, 1, inner + 1, axis=axis_index)
    return block


def build_transfer_array(neighbour_image_block):
    return jnp.concatenate(
        [class_fold(neighbour_image_block, members) for members in fold_classes()], axis=3
    )


def collect_back(incoming_atoms, width):
    summed = None
    for index, members in enumerate(fold_classes()):
        piece = class_fold(incoming_atoms[..., index * width : (index + 1) * width], members)
        summed = piece if summed is None else summed + piece
    return summed


def row_of(array, index):
    return lax.dynamic_index_in_dim(array, index, 0, keepdims=False)


def put_row(array, index, value):
    return lax.dynamic_update_index_in_dim(array, value, index, 0)


def add_row(array, index, value):
    return put_row(array, index, row_of(array, index) + value)


def body(positions, types):
    cell_count_first, cells_y, cells_z, slots = types.shape
    weight, embedding = type_tables(types)
    payload = jnp.concatenate([positions, weight], axis=3)
    padded = padded_2(payload, (("gx", 0), ("gy", 1), ("gz", 2)), 1)
    pad_coords = padded[..., : 3 * slots].reshape(
        cell_count_first + 2, cells_y + 2, cells_z + 2, 3, slots
    )
    pad_weight = padded[..., 3 * slots :]
    own_coords = positions.reshape(cell_count_first, cells_y, cells_z, 3, slots)
    slot_ids = lax.broadcasted_iota(jnp.int32, (slots, slots), 0)
    pair_ids = lax.broadcasted_iota(jnp.int32, (slots, slots), 1)
    ordered = jnp.where(slot_ids < pair_ids, 1.0, 0.0).astype(jnp.float32)

    def window(array, plane, cell_shift):
        layer = row_of(array, plane + 1 + cell_shift[0])
        return layer[
            1 + cell_shift[1] : 1 + cell_shift[1] + cells_y,
            1 + cell_shift[2] : 1 + cell_shift[2] + cells_z,
        ]

    def place(array, cell_shift):
        widths = (
            (1 + cell_shift[1], 1 - cell_shift[1]),
            (1 + cell_shift[2], 1 - cell_shift[2]),
        ) + ((0, 0),) * (array.ndim - 2)
        return jnp.pad(array, widths)

    def half_density_step(plane, carry):
        own_part, image_portion = carry
        plane_coords = row_of(own_coords, plane)
        plane_weight = row_of(weight, plane)
        summed = jnp.zeros((cells_y, cells_z, slots), jnp.float32)
        for cell_shift in half_shifts():
            displace, square = separation(
                plane_coords, window(pad_coords, plane, cell_shift), cell_shift
            )
            dens = density_shape(square)
            if cell_shift == (0, 0, 0):
                dens = dens * ordered
            summed = summed + jnp.sum(
                dens * window(pad_weight, plane, cell_shift)[..., None, :], axis=-1
            )
            image_portion = add_row(
                image_portion,
                plane + 1 + cell_shift[0],
                place(jnp.sum(dens * plane_weight[..., :, None], axis=-2), cell_shift),
            )
        return (put_row(own_part, plane, summed), image_portion)

    start = (
        jnp.zeros((cell_count_first, cells_y, cells_z, slots), jnp.float32),
        jnp.zeros((cell_count_first + 2, cells_y + 2, cells_z + 2, slots), jnp.float32),
    )
    own_part, image_portion = lax.fori_loop(0, cell_count_first, half_density_step, start)
    incoming_atoms = padded_2(
        build_transfer_array(image_portion), (("gx", 0), ("gy", 1), ("gz", 2)), 1
    )
    density_sum = own_part + image_portion[1:-1, 1:-1, 1:-1] + collect_back(incoming_atoms, slots)
    root_value = jnp.sqrt(density_sum + 1.0)
    slope = -embedding / (2.0 * root_value)
    pad_slope = padded_2(slope, (("gx", 0), ("gy", 1), ("gz", 2)), 1)

    def pair_terms(plane, cell_shift):
        plane_weight = row_of(weight, plane)
        plane_slope = row_of(slope, plane)
        other_weight = window(pad_weight, plane, cell_shift)
        other_slope = window(pad_slope, plane, cell_shift)
        displace, square = separation(
            row_of(own_coords, plane), window(pad_coords, plane, cell_shift), cell_shift
        )
        dens_slope, pair_value, pair_slope = all_shapes(square)
        both_weight = plane_weight[..., :, None] * other_weight[..., None, :]
        coupling = (
            plane_slope[..., :, None] * other_weight[..., None, :]
            + other_slope[..., None, :] * plane_weight[..., :, None]
        ) * dens_slope + 0.5 * both_weight * pair_slope
        return (displace, coupling, 0.25 * both_weight * pair_value)

    emb_energy = -embedding * root_value
    force_start = jnp.zeros((cell_count_first, cells_y, cells_z, 3, slots), jnp.float32)
    pair_start = jnp.zeros((cell_count_first, cells_y, cells_z, slots), jnp.float32)

    def half_force_step(plane, carry):
        force_all, pair_all, image_portion = carry
        force_sum = jnp.zeros((cells_y, cells_z, 3, slots), jnp.float32)
        pair_sum = jnp.zeros((cells_y, cells_z, slots), jnp.float32)
        for cell_shift in half_shifts():
            displace, coupling, energy_pair = pair_terms(plane, cell_shift)
            if cell_shift == (0, 0, 0):
                coupling = coupling * ordered
                energy_pair = energy_pair * ordered
            pair_force = 2.0 * coupling[..., None, :, :] * displace
            force_sum = force_sum + jnp.sum(pair_force, axis=-1)
            pair_sum = pair_sum + jnp.sum(energy_pair, axis=-1)
            partner = jnp.concatenate(
                [-jnp.sum(pair_force, axis=-2), jnp.sum(energy_pair, axis=-2)[..., None, :]],
                axis=-2,
            )
            image_portion = add_row(
                image_portion, plane + 1 + cell_shift[0], place(partner, cell_shift)
            )
        return (
            put_row(force_all, plane, force_sum),
            put_row(pair_all, plane, pair_sum),
            image_portion,
        )

    image_start = jnp.zeros((cell_count_first + 2, cells_y + 2, cells_z + 2, 4, slots), jnp.float32)
    force_all, pair_all, image_portion = lax.fori_loop(
        0, cell_count_first, half_force_step, (force_start, pair_start, image_start)
    )
    image_flattened = image_portion.reshape(
        cell_count_first + 2, cells_y + 2, cells_z + 2, 4 * slots
    )
    incoming_atoms = padded_2(
        build_transfer_array(image_flattened), (("gx", 0), ("gy", 1), ("gz", 2)), 1
    )
    own_flat = jnp.concatenate(
        [force_all.reshape(cell_count_first, cells_y, cells_z, 3 * slots), pair_all + emb_energy],
        axis=-1,
    )
    return own_flat + image_flattened[1:-1, 1:-1, 1:-1] + collect_back(incoming_atoms, 4 * slots)


def solution(mesh):
    in_specs = (P("gx", "gy", "gz", None), P("gx", "gy", "gz", None))
    out_specs = P("gx", "gy", "gz", None)
    return jax.shard_map(body, mesh=mesh, in_specs=in_specs, out_specs=out_specs, check_vma=False)
```

profile of v0, /device:TPU:0, one launch (start us, length us, event | category | flops | bytes accessed | tf_op | source)
XLA Modules:
  0.0 152.7 jit_solution(15879694539840778715)
XLA Ops:
  1.6 3.0 %collective-permute-start = (f32[1,3,8,128]{3,2,1,0:T(8,128)S(1)}, f32[1,3,8,128]{3,2,1,0:T(8,128)S(1)}, u32[]{:S(2)}, u32[]{:S(2)}) collective-permute-start(f32[1,3,8,128]{3,2,1,0:T(8,128)S(1)} %get-tuple-element.2066), channel_id=1, source_target_pairs={{0,8},{8,16},{16,24},{24,0},{1,9},{9,17},{17,25},{25,1},{2,10},{10... | collective-permute-start | bytes 36872 | tf_op jit(solution)/shard_map/ppermute | solution.py:18
  10.6 2.2 %collective-permute-start.3 = (f32[5,1,8,128]{3,2,1,0:T(8,128)S(1)}, f32[5,1,8,128]{3,2,1,0:T(8,128)S(1)}, u32[]{:S(2)}, u32[]{:S(2)}) collective-permute-start(f32[5,1,8,128]{3,2,1,0:T(8,128)S(1)} %get-tuple-element.2046), channel_id=1, source_target_pairs={{2,0},{4,2},{6,4},{0,6},{3,1},{5,3},{7,5},{1,7},{10,8},{12,10},{14... | collective-permute-start | bytes 61448 | tf_op jit(solution)/shard_map/ppermute | solution.py:19
  18.0 23.6 %while.45 = (s32[]{:T(128)}, f32[3,3,8,32]{3,2,1,0:T(8,128)S(1)}, f32[5,5,10,32]{3,2,1,0:T(8,128)S(1)}, f32[5,5,10,3,32]{4,3,2,1,0:T(4,128)S(1)}, f32[3,3,8,3,32...) while((s32[]{:T(128)}, f32[3,3,8,32]{3,2,1,0:T(8,128)S(1)}, ...), condition=%wide.region_43.44_spmd.clone.clone, body=%wide.region_0.43_spmd.sunk.clone.clone.sunk | while | flops 6260617 | bytes 5239377 | solution.py:157
  18.4 3.6 %multiply_reduce_fusion.45 = (f32[3,8,32,32]{3,2,1,0:T(8,128)S(1)}, f32[3,8,32,32]{3,2,1,0:T(8,128)S(1)}, f32[3,8,32,32]{3,2,1,0:T(8,128)S(1)}, f32[3,8,32,32]{3...) fusion(f32[3,8,3,32]{3,2,1,0:T(4,128)S(1)} %get-tuple-element.2, ...), kind=kLoop, calls=%fused_computation.14.clone.1 | loop fusion | flops 2752512 | bytes 1514496 | tf_op jit(solution)/shard_map/while/body/eval_jaxpr/reduce_sum | solution.py:33
  23.3 2.1 %multiply_reduce_fusion.46 = (f32[3,8,32]{2,1,0:T(8,128)S(1)}, f32[3,8,32]{2,1,0:T(8,128)S(1)}, f32[3,8,32]{2,1,0:T(8,128)S(1)}, f32[3,8,32]{2,1,0:T(8,128)S(1)}...) fusion(f32[3,8,32,32]{3,2,1,0:T(8,128)S(1)} %get-tuple-element., ...), kind=kLoop, calls=%fused_computation.31.clone.1 | loop fusion | flops 2198016 | bytes 970752 | tf_op jit(solution)/shard_map/while/body/eval_jaxpr/reduce_sum | solution.py:149
  26.3 3.6 %multiply_reduce_fusion.45 = (f32[3,8,32,32]{3,2,1,0:T(8,128)S(1)}, f32[3,8,32,32]{3,2,1,0:T(8,128)S(1)}, f32[3,8,32,32]{3,2,1,0:T(8,128)S(1)}, f32[3,8,32,32]{3...) fusion(f32[3,8,3,32]{3,2,1,0:T(4,128)S(1)} %get-tuple-element.2, ...), kind=kLoop, calls=%fused_computation.14.clone.1 | loop fusion | flops 2752512 | bytes 1514496 | tf_op jit(solution)/shard_map/while/body/eval_jaxpr/reduce_sum | solution.py:33
  31.2 2.1 %multiply_reduce_fusion.46 = (f32[3,8,32]{2,1,0:T(8,128)S(1)}, f32[3,8,32]{2,1,0:T(8,128)S(1)}, f32[3,8,32]{2,1,0:T(8,128)S(1)}, f32[3,8,32]{2,1,0:T(8,128)S(1)}...) fusion(f32[3,8,32,32]{3,2,1,0:T(8,128)S(1)} %get-tuple-element., ...), kind=kLoop, calls=%fused_computation.31.clone.1 | loop fusion | flops 2198016 | bytes 970752 | tf_op jit(solution)/shard_map/while/body/eval_jaxpr/reduce_sum | solution.py:149
  34.2 3.6 %multiply_reduce_fusion.45 = (f32[3,8,32,32]{3,2,1,0:T(8,128)S(1)}, f32[3,8,32,32]{3,2,1,0:T(8,128)S(1)}, f32[3,8,32,32]{3,2,1,0:T(8,128)S(1)}, f32[3,8,32,32]{3...) fusion(f32[3,8,3,32]{3,2,1,0:T(4,128)S(1)} %get-tuple-element.2, ...), kind=kLoop, calls=%fused_computation.14.clone.1 | loop fusion | flops 2752512 | bytes 1514496 | tf_op jit(solution)/shard_map/while/body/eval_jaxpr/reduce_sum | solution.py:33
  39.1 2.1 %multiply_reduce_fusion.46 = (f32[3,8,32]{2,1,0:T(8,128)S(1)}, f32[3,8,32]{2,1,0:T(8,128)S(1)}, f32[3,8,32]{2,1,0:T(8,128)S(1)}, f32[3,8,32]{2,1,0:T(8,128)S(1)}...) fusion(f32[3,8,32,32]{3,2,1,0:T(8,128)S(1)} %get-tuple-element., ...), kind=kLoop, calls=%fused_computation.31.clone.1 | loop fusion | flops 2198016 | bytes 970752 | tf_op jit(solution)/shard_map/while/body/eval_jaxpr/reduce_sum | solution.py:149
  42.2 2.4 %collective-permute-start.6 = (f32[1,3,8,224]{3,2,1,0:T(8,128)S(1)}, f32[1,3,8,224]{3,2,1,0:T(8,128)S(1)}, u32[]{:S(2)}, u32[]{:S(2)}) collective-permute-start(f32[1,3,8,224]{3,2,1,0:T(8,128)S(1)} %get-tuple-element.2060), channel_id=1, source_target_pairs={{0,8},{8,16},{16,24},{24,0},{1,9},{9,17},{17,25},{25,1},{2,10},{10... | collective-permute-start | bytes 64520 | tf_op jit(solution)/shard_map/ppermute | solution.py:18
  49.9 2.5 %collective-permute-start.9 = (f32[5,1,8,224]{3,2,1,0:T(8,128)S(1)}, f32[5,1,8,224]{3,2,1,0:T(8,128)S(1)}, u32[]{:S(2)}, u32[]{:S(2)}) collective-permute-start(f32[5,1,8,224]{3,2,1,0:T(8,128)S(1)} %get-tuple-element.2038), channel_id=1, source_target_pairs={{2,0},{4,2},{6,4},{0,6},{3,1},{5,3},{7,5},{1,7},{10,8},{12,10},{14... | collective-permute-start | bytes 107528 | tf_op jit(solution)/shard_map/ppermute | solution.py:19
  52.5 2.0 %collective-permute-done.8 = f32[5,1,8,224]{3,2,1,0:T(8,128)S(1)} collective-permute-done((f32[5,1,8,224]{3,2,1,0:T(8,128)S(1)}, f32[5,1,8,224]{3,2,1,0:T(8,128)S(1)}, u32[]{:S(2)}, u32[]{:S(2)}) %collective-permute-start.8) | collective-permute-done | bytes 35872 | tf_op jit(solution)/shard_map/ppermute | solution.py:18
  63.1 2.8 %collective-permute-start.15 = (f32[5,1,8,32]{3,2,1,0:T(8,128)S(1)}, f32[5,1,8,32]{3,2,1,0:T(8,128)S(1)}, u32[]{:S(2)}, u32[]{:S(2)}) collective-permute-start(f32[5,1,8,32]{3,2,1,0:T(8,128)S(1)} %get-tuple-element.2069), channel_id=1, source_target_pairs={{2,0},{4,2},{6,4},{0,6},{3,1},{5,3},{7,5},{1,7},{10,8},{12,10},{14... | collective-permute-start | bytes 15368 | tf_op jit(solution)/shard_map/ppermute | solution.py:19
  69.4 63.5 %while.46 = (s32[]{:T(128)}, f32[3,3,8,3,32]{4,3,2,1,0:T(4,128)S(1)}, f32[3,3,8,32]{3,2,1,0:T(8,128)S(1)}, f32[5,5,10,4,32]{4,3,2,1,0:T(4,128)S(1)}, f32[3,3,8,3...) while((s32[]{:T(128)}, ...), condition=%wide.region_115.116_spmd.clone.clone.clone, body=%wide.region_44.115_spmd.sunk.clone.clone.clone.sunk | while | flops 19310856 | bytes 13459565 | solution.py:212
  71.2 4.0 %fusion.356 = (f32[3,8,3,32]{3,2,1,0:T(4,128)S(1)}, f32[3,8,3,32]{3,2,1,0:T(4,128)S(1)}, f32[3,8,32,32]{3,2,1,0:T(8,128)S(1)}, f32[3,8,32,32]{3,2,1,0:T(8,128)S(...) fusion(f32[3,8,32,32]{3,2,1,0:T(8,128)S(1)} %get-tuple-element., ...), kind=kLoop, calls=%fused_computation.179.clone.1 | loop fusion | flops 2939904 | bytes 1551360 | tf_op jit(solution)/shard_map/while/body/eval_jaxpr/reduce_sum | solution.py:199
  77.1 3.1 %fusion.361 = (f32[3,8,32]{2,1,0:T(8,128)S(1)}, f32[3,8,32]{2,1,0:T(8,128)S(1)}, f32[3,8,32]{2,1,0:T(8,128)S(1)}, f32[3,8,32]{2,1,0:T(8,128)S(1)}, f32[3,8,32]{2...) fusion(f32[3,8,32,32]{3,2,1,0:T(8,128)S(1)} %get-tuple-element., ...), kind=kLoop, calls=%fused_computation.329.clone.1 | loop fusion | flops 3947520 | bytes 1158144 | tf_op jit(solution)/shard_map/while/body/eval_jaxpr/reduce_sum | solution.py:199
  80.3 1.9 %fusion.360 = (f32[3,8,32,32]{3,2,1,0:T(8,128)S(1)}, f32[3,8,32,32]{3,2,1,0:T(8,128)S(1)}, f32[3,8,32,32]{3,2,1,0:T(8,128)S(1)}, f32[3,8,32,32]{3,2,1,0:T(8,128)S(1)}, f32[3,8,32,32]{3,2,1,0:T(8,128)S(1)}) fusion(f32[3,8,32,32]{3,2,1,0:T(8,128)S(1)} %get-tuple-element.2527, f32[3,8,32]{2,1,0:T(8,128)S(1)} %get-tuple-element.2529, ...), kind=kLoop, calls=%fused_computation.265.clone.1 | loop fusion | flops 2949120 | bytes 1019904 | tf_op jit(solution)/shard_map/while/body/eval_jaxpr/mul | solution.py:195
  82.9 4.2 %fusion.362 = (f32[3,8,3,32]{3,2,1,0:T(4,128)S(1)}, f32[3,8,3,32]{3,2,1,0:T(4,128)S(1)}, f32[3,8,3,32]{3,2,1,0:T(4,128)S(1)}, f32[3,8,3,32]{3,2,1,0:T(4,128)S(1)...) fusion(f32[3,8,32,32]{3,2,1,0:T(8,128)S(1)} %get-tuple-element., ...), kind=kLoop, calls=%fused_computation.177.clone.1 | loop fusion | flops 2612736 | bytes 1142784 | tf_op jit(solution)/shard_map/while/body/eval_jaxpr/reduce_sum | solution.py:199
  87.9 2.1 %fusion.363 = (f32[3,8,3,32]{3,2,1,0:T(4,128)S(1)}, f32[3,8,3,32]{3,2,1,0:T(4,128)S(1)}, f32[3,8,3,32]{3,2,1,0:T(4,128)S(1)}, f32[3,8,3,32]{3,2,1,0:T(4,128)S(1)...) fusion(f32[3,8,32,32]{3,2,1,0:T(8,128)S(1)} %get-tuple-element.2567, ...), kind=kLoop, calls=%fused_computation.175.clone.1 | loop fusion | flops 870912 | bytes 387072 | tf_op jit(solution)/shard_map/while/body/eval_jaxpr/reduce_sum | solution.py:199
  92.3 4.0 %fusion.356 = (f32[3,8,3,32]{3,2,1,0:T(4,128)S(1)}, f32[3,8,3,32]{3,2,1,0:T(4,128)S(1)}, f32[3,8,32,32]{3,2,1,0:T(8,128)S(1)}, f32[3,8,32,32]{3,2,1,0:T(8,128)S(...) fusion(f32[3,8,32,32]{3,2,1,0:T(8,128)S(1)} %get-tuple-element., ...), kind=kLoop, calls=%fused_computation.179.clone.1 | loop fusion | flops 2939904 | bytes 1551360 | tf_op jit(solution)/shard_map/while/body/eval_jaxpr/reduce_sum | solution.py:199
  98.3 3.1 %fusion.361 = (f32[3,8,32]{2,1,0:T(8,128)S(1)}, f32[3,8,32]{2,1,0:T(8,128)S(1)}, f32[3,8,32]{2,1,0:T(8,128)S(1)}, f32[3,8,32]{2,1,0:T(8,128)S(1)}, f32[3,8,32]{2...) fusion(f32[3,8,32,32]{3,2,1,0:T(8,128)S(1)} %get-tuple-element., ...), kind=kLoop, calls=%fused_computation.329.clone.1 | loop fusion | flops 3947520 | bytes 1158144 | tf_op jit(solution)/shard_map/while/body/eval_jaxpr/reduce_sum | solution.py:199
  101.4 1.9 %fusion.360 = (f32[3,8,32,32]{3,2,1,0:T(8,128)S(1)}, f32[3,8,32,32]{3,2,1,0:T(8,128)S(1)}, f32[3,8,32,32]{3,2,1,0:T(8,128)S(1)}, f32[3,8,32,32]{3,2,1,0:T(8,128)S(1)}, f32[3,8,32,32]{3,2,1,0:T(8,128)S(1)}) fusion(f32[3,8,32,32]{3,2,1,0:T(8,128)S(1)} %get-tuple-element.2527, f32[3,8,32]{2,1,0:T(8,128)S(1)} %get-tuple-element.2529, ...), kind=kLoop, calls=%fused_computation.265.clone.1 | loop fusion | flops 2949120 | bytes 1019904 | tf_op jit(solution)/shard_map/while/body/eval_jaxpr/mul | solution.py:195
  104.1 4.2 %fusion.362 = (f32[3,8,3,32]{3,2,1,0:T(4,128)S(1)}, f32[3,8,3,32]{3,2,1,0:T(4,128)S(1)}, f32[3,8,3,32]{3,2,1,0:T(4,128)S(1)}, f32[3,8,3,32]{3,2,1,0:T(4,128)S(1)...) fusion(f32[3,8,32,32]{3,2,1,0:T(8,128)S(1)} %get-tuple-element., ...), kind=kLoop, calls=%fused_computation.177.clone.1 | loop fusion | flops 2612736 | bytes 1142784 | tf_op jit(solution)/shard_map/while/body/eval_jaxpr/reduce_sum | solution.py:199
  109.1 2.1 %fusion.363 = (f32[3,8,3,32]{3,2,1,0:T(4,128)S(1)}, f32[3,8,3,32]{3,2,1,0:T(4,128)S(1)}, f32[3,8,3,32]{3,2,1,0:T(4,128)S(1)}, f32[3,8,3,32]{3,2,1,0:T(4,128)S(1)...) fusion(f32[3,8,32,32]{3,2,1,0:T(8,128)S(1)} %get-tuple-element.2567, ...), kind=kLoop, calls=%fused_computation.175.clone.1 | loop fusion | flops 870912 | bytes 387072 | tf_op jit(solution)/shard_map/while/body/eval_jaxpr/reduce_sum | solution.py:199
  113.5 4.0 %fusion.356 = (f32[3,8,3,32]{3,2,1,0:T(4,128)S(1)}, f32[3,8,3,32]{3,2,1,0:T(4,128)S(1)}, f32[3,8,32,32]{3,2,1,0:T(8,128)S(1)}, f32[3,8,32,32]{3,2,1,0:T(8,128)S(...) fusion(f32[3,8,32,32]{3,2,1,0:T(8,128)S(1)} %get-tuple-element., ...), kind=kLoop, calls=%fused_computation.179.clone.1 | loop fusion | flops 2939904 | bytes 1551360 | tf_op jit(solution)/shard_map/while/body/eval_jaxpr/reduce_sum | solution.py:199
  119.4 3.1 %fusion.361 = (f32[3,8,32]{2,1,0:T(8,128)S(1)}, f32[3,8,32]{2,1,0:T(8,128)S(1)}, f32[3,8,32]{2,1,0:T(8,128)S(1)}, f32[3,8,32]{2,1,0:T(8,128)S(1)}, f32[3,8,32]{2...) fusion(f32[3,8,32,32]{3,2,1,0:T(8,128)S(1)} %get-tuple-element., ...), kind=kLoop, calls=%fused_computation.329.clone.1 | loop fusion | flops 3947520 | bytes 1158144 | tf_op jit(solution)/shard_map/while/body/eval_jaxpr/reduce_sum | solution.py:199
  122.5 1.9 %fusion.360 = (f32[3,8,32,32]{3,2,1,0:T(8,128)S(1)}, f32[3,8,32,32]{3,2,1,0:T(8,128)S(1)}, f32[3,8,32,32]{3,2,1,0:T(8,128)S(1)}, f32[3,8,32,32]{3,2,1,0:T(8,128)S(1)}, f32[3,8,32,32]{3,2,1,0:T(8,128)S(1)}) fusion(f32[3,8,32,32]{3,2,1,0:T(8,128)S(1)} %get-tuple-element.2527, f32[3,8,32]{2,1,0:T(8,128)S(1)} %get-tuple-element.2529, ...), kind=kLoop, calls=%fused_computation.265.clone.1 | loop fusion | flops 2949120 | bytes 1019904 | tf_op jit(solution)/shard_map/while/body/eval_jaxpr/mul | solution.py:195
  125.2 4.2 %fusion.362 = (f32[3,8,3,32]{3,2,1,0:T(4,128)S(1)}, f32[3,8,3,32]{3,2,1,0:T(4,128)S(1)}, f32[3,8,3,32]{3,2,1,0:T(4,128)S(1)}, f32[3,8,3,32]{3,2,1,0:T(4,128)S(1)...) fusion(f32[3,8,32,32]{3,2,1,0:T(8,128)S(1)} %get-tuple-element., ...), kind=kLoop, calls=%fused_computation.177.clone.1 | loop fusion | flops 2612736 | bytes 1142784 | tf_op jit(solution)/shard_map/while/body/eval_jaxpr/reduce_sum | solution.py:199
  130.2 2.1 %fusion.363 = (f32[3,8,3,32]{3,2,1,0:T(4,128)S(1)}, f32[3,8,3,32]{3,2,1,0:T(4,128)S(1)}, f32[3,8,3,32]{3,2,1,0:T(4,128)S(1)}, f32[3,8,3,32]{3,2,1,0:T(4,128)S(1)...) fusion(f32[3,8,32,32]{3,2,1,0:T(8,128)S(1)} %get-tuple-element.2567, ...), kind=kLoop, calls=%fused_computation.175.clone.1 | loop fusion | flops 870912 | bytes 387072 | tf_op jit(solution)/shard_map/while/body/eval_jaxpr/reduce_sum | solution.py:199
  137.4 3.0 %collective-permute-done.18 = f32[1,3,8,896]{3,2,1,0:T(8,128)S(1)} collective-permute-done((f32[1,3,8,896]{3,2,1,0:T(8,128)S(1)}, f32[1,3,8,896]{3,2,1,0:T(8,128)S(1)}, u32[]{:S(2)}, u32[]{:S(2)}) %collective-permute-start.18) | collective-permute-done | bytes 86048 | tf_op jit(solution)/shard_map/ppermute | solution.py:18
  141.8 2.7 %collective-permute-start.21 = (f32[5,1,8,896]{3,2,1,0:T(8,128)S(1)}, f32[5,1,8,896]{3,2,1,0:T(8,128)S(1)}, u32[]{:S(2)}, u32[]{:S(2)}) collective-permute-start(f32[5,1,8,896]{3,2,1,0:T(8,128)S(1)} %get-tuple-element.1993), channel_id=1, source_target_pairs={{2,0},{4,2},{6,4},{0,6},{3,1},{5,3},{7,5},{1,7},{10,8},{12,10},{14... | collective-permute-start | bytes 430088 | tf_op jit(solution)/shard_map/ppermute | solution.py:19
  144.6 4.6 %collective-permute-done.20 = f32[5,1,8,896]{3,2,1,0:T(8,128)S(1)} collective-permute-done((f32[5,1,8,896]{3,2,1,0:T(8,128)S(1)}, f32[5,1,8,896]{3,2,1,0:T(8,128)S(1)}, u32[]{:S(2)}, u32[]{:S(2)}) %collective-permute-start.20) | collective-permute-done | bytes 143392 | tf_op jit(solution)/shard_map/ppermute | solution.py:18
  (457 shorter events, 61.6 us)
Async XLA Ops:
  0.0 16.2 %copy-start = (f32[3,3,8,96]{3,2,1,0:T(8,128)S(1)}, f32[3,3,8,96]{3,2,1,0:T(8,128)}, u32[]{:S(2)}) copy-start(f32[3,3,8,96]{3,2,1,0:T(8,128)} %param.34) | copy-start | bytes 82948
  1.6 5.6 %collective-permute-start = (f32[1,3,8,128]{3,2,1,0:T(8,128)S(1)}, f32[1,3,8,128]{3,2,1,0:T(8,128)S(1)}, u32[]{:S(2)}, u32[]{:S(2)}) collective-permute-start(f32[1,3,8,128]{3,2,1,0:T(8,128)S(1)} %get-tuple-element.2066), channel_id=1, source_target_pairs={{0,8},{8,16},{16,24},{24,0},{1,9},{9,17},{17,25},{25,1},{2,10},{10... | collective-permute-start | bytes 36872 | tf_op jit(solution)/shard_map/ppermute | solution.py:18
  4.6 3.7 %collective-permute-start.1 = (f32[1,3,8,128]{3,2,1,0:T(8,128)S(1)}, f32[1,3,8,128]{3,2,1,0:T(8,128)S(1)}, u32[]{:S(2)}, u32[]{:S(2)}) collective-permute-start(f32[1,3,8,128]{3,2,1,0:T(8,128)S(1)} %get-tuple-element.2067), channel_id=1, source_target_pairs={{8,0},{16,8},{24,16},{0,24},{9,1},{17,9},{25,17},{1,25},{10,2},{18... | collective-permute-start | bytes 36872 | tf_op jit(solution)/shard_map/ppermute | solution.py:19
  9.1 5.6 %collective-permute-start.2 = (f32[5,1,8,128]{3,2,1,0:T(8,128)S(1)}, f32[5,1,8,128]{3,2,1,0:T(8,128)S(1)}, u32[]{:S(2)}, u32[]{:S(2)}) collective-permute-start(f32[5,1,8,128]{3,2,1,0:T(8,128)S(1)} %get-tuple-element.2045), channel_id=1, source_target_pairs={{0,2},{2,4},{4,6},{6,0},{1,3},{3,5},{5,7},{7,1},{8,10},{10,12},{12... | collective-permute-start | bytes 61448 | tf_op jit(solution)/shard_map/ppermute | solution.py:18
  10.6 4.0 %collective-permute-start.3 = (f32[5,1,8,128]{3,2,1,0:T(8,128)S(1)}, f32[5,1,8,128]{3,2,1,0:T(8,128)S(1)}, u32[]{:S(2)}, u32[]{:S(2)}) collective-permute-start(f32[5,1,8,128]{3,2,1,0:T(8,128)S(1)} %get-tuple-element.2046), channel_id=1, source_target_pairs={{2,0},{4,2},{6,4},{0,6},{3,1},{5,3},{7,5},{1,7},{10,8},{12,10},{14... | collective-permute-start | bytes 61448 | tf_op jit(solution)/shard_map/ppermute | solution.py:19
  15.6 1.2 collective-permute-start.4
  15.7 1.3 collective-permute-start.5
  17.3 0.7 copy-start.6
  17.3 0.7 copy-start.7
  17.3 0.7 copy-start.8
  17.3 0.7 copy-start.9
  17.3 0.7 copy-start.10
  17.3 0.7 copy-start.11
  17.4 0.7 copy-start.12
  42.2 4.8 %collective-permute-start.6 = (f32[1,3,8,224]{3,2,1,0:T(8,128)S(1)}, f32[1,3,8,224]{3,2,1,0:T(8,128)S(1)}, u32[]{:S(2)}, u32[]{:S(2)}) collective-permute-start(f32[1,3,8,224]{3,2,1,0:T(8,128)S(1)} %get-tuple-element.2060), channel_id=1, source_target_pairs={{0,8},{8,16},{16,24},{24,0},{1,9},{9,17},{17,25},{25,1},{2,10},{10... | collective-permute-start | bytes 64520 | tf_op jit(solution)/shard_map/ppermute | solution.py:18
  44.7 3.8 %collective-permute-start.7 = (f32[1,3,8,224]{3,2,1,0:T(8,128)S(1)}, f32[1,3,8,224]{3,2,1,0:T(8,128)S(1)}, u32[]{:S(2)}, u32[]{:S(2)}) collective-permute-start(f32[1,3,8,224]{3,2,1,0:T(8,128)S(1)} %get-tuple-element.2061), channel_id=1, source_target_pairs={{8,0},{16,8},{24,16},{0,24},{9,1},{17,9},{25,17},{1,25},{10,2},{18... | collective-permute-start | bytes 64520 | tf_op jit(solution)/shard_map/ppermute | solution.py:19
  48.5 6.0 %collective-permute-start.8 = (f32[5,1,8,224]{3,2,1,0:T(8,128)S(1)}, f32[5,1,8,224]{3,2,1,0:T(8,128)S(1)}, u32[]{:S(2)}, u32[]{:S(2)}) collective-permute-start(f32[5,1,8,224]{3,2,1,0:T(8,128)S(1)} %get-tuple-element.2037), channel_id=1, source_target_pairs={{0,2},{2,4},{4,6},{6,0},{1,3},{3,5},{5,7},{7,1},{8,10},{10,12},{12... | collective-permute-start | bytes 107528 | tf_op jit(solution)/shard_map/ppermute | solution.py:18
  49.9 4.6 %collective-permute-start.9 = (f32[5,1,8,224]{3,2,1,0:T(8,128)S(1)}, f32[5,1,8,224]{3,2,1,0:T(8,128)S(1)}, u32[]{:S(2)}, u32[]{:S(2)}) collective-permute-start(f32[5,1,8,224]{3,2,1,0:T(8,128)S(1)} %get-tuple-element.2038), channel_id=1, source_target_pairs={{2,0},{4,2},{6,4},{0,6},{3,1},{5,3},{7,5},{1,7},{10,8},{12,10},{14... | collective-permute-start | bytes 107528 | tf_op jit(solution)/shard_map/ppermute | solution.py:19
  54.5 1.3 collective-permute-start.10
  54.6 1.3 collective-permute-start.11
  56.8 4.6 %collective-permute-start.12 = (f32[1,3,8,32]{3,2,1,0:T(8,128)S(1)}, f32[1,3,8,32]{3,2,1,0:T(8,128)S(1)}, u32[]{:S(2)}, u32[]{:S(2)}) collective-permute-start(f32[1,3,8,32]{3,2,1,0:T(8,128)S(1)} %get-tuple-element.2070), channel_id=1, source_target_pairs={{0,8},{8,16},{16,24},{24,0},{1,9},{9,17},{17,25},{25,1},{2,10},{10... | collective-permute-start | bytes 9224 | tf_op jit(solution)/shard_map/ppermute | solution.py:18
  58.4 3.7 %collective-permute-start.13 = (f32[1,3,8,32]{3,2,1,0:T(8,128)S(1)}, f32[1,3,8,32]{3,2,1,0:T(8,128)S(1)}, u32[]{:S(2)}, u32[]{:S(2)}) collective-permute-start(f32[1,3,8,32]{3,2,1,0:T(8,128)S(1)} %get-tuple-element.2071), channel_id=1, source_target_pairs={{8,0},{16,8},{24,16},{0,24},{9,1},{17,9},{25,17},{1,25},{10,2},{18... | collective-permute-start | bytes 9224 | tf_op jit(solution)/shard_map/ppermute | solution.py:19
  62.1 5.7 %collective-permute-start.14 = (f32[5,1,8,32]{3,2,1,0:T(8,128)S(1)}, f32[5,1,8,32]{3,2,1,0:T(8,128)S(1)}, u32[]{:S(2)}, u32[]{:S(2)}) collective-permute-start(f32[5,1,8,32]{3,2,1,0:T(8,128)S(1)} %get-tuple-element.2068), channel_id=1, source_target_pairs={{0,2},{2,4},{4,6},{6,0},{1,3},{3,5},{5,7},{7,1},{8,10},{10,12},{12... | collective-permute-start | bytes 15368 | tf_op jit(solution)/shard_map/ppermute | solution.py:18
  63.1 4.7 %collective-permute-start.15 = (f32[5,1,8,32]{3,2,1,0:T(8,128)S(1)}, f32[5,1,8,32]{3,2,1,0:T(8,128)S(1)}, u32[]{:S(2)}, u32[]{:S(2)}) collective-permute-start(f32[5,1,8,32]{3,2,1,0:T(8,128)S(1)} %get-tuple-element.2069), channel_id=1, source_target_pairs={{2,0},{4,2},{6,4},{0,6},{3,1},{5,3},{7,5},{1,7},{10,8},{12,10},{14... | collective-permute-start | bytes 15368 | tf_op jit(solution)/shard_map/ppermute | solution.py:19
  67.8 1.2 collective-permute-start.16
  67.9 1.3 collective-permute-start.17
  134.0 6.4 %collective-permute-start.18 = (f32[1,3,8,896]{3,2,1,0:T(8,128)S(1)}, f32[1,3,8,896]{3,2,1,0:T(8,128)S(1)}, u32[]{:S(2)}, u32[]{:S(2)}) collective-permute-start(f32[1,3,8,896]{3,2,1,0:T(8,128)S(1)} %get-tuple-element.2002), channel_id=1, source_target_pairs={{0,8},{8,16},{16,24},{24,0},{1,9},{9,17},{17,25},{25,1},{2,10},{10... | collective-permute-start | bytes 258056 | tf_op jit(solution)/shard_map/ppermute | solution.py:18
  135.2 5.5 %collective-permute-start.19 = (f32[1,3,8,896]{3,2,1,0:T(8,128)S(1)}, f32[1,3,8,896]{3,2,1,0:T(8,128)S(1)}, u32[]{:S(2)}, u32[]{:S(2)}) collective-permute-start(f32[1,3,8,896]{3,2,1,0:T(8,128)S(1)} %get-tuple-element.2003), channel_id=1, source_target_pairs={{8,0},{16,8},{24,16},{0,24},{9,1},{17,9},{25,17},{1,25},{10,2},{18... | collective-permute-start | bytes 258056 | tf_op jit(solution)/shard_map/ppermute | solution.py:19
  140.7 8.5 %collective-permute-start.20 = (f32[5,1,8,896]{3,2,1,0:T(8,128)S(1)}, f32[5,1,8,896]{3,2,1,0:T(8,128)S(1)}, u32[]{:S(2)}, u32[]{:S(2)}) collective-permute-start(f32[5,1,8,896]{3,2,1,0:T(8,128)S(1)} %get-tuple-element.1992), channel_id=1, source_target_pairs={{0,2},{2,4},{4,6},{6,0},{1,3},{3,5},{5,7},{7,1},{8,10},{10,12},{12... | collective-permute-start | bytes 430088 | tf_op jit(solution)/shard_map/ppermute | solution.py:18
  141.8 8.1 %collective-permute-start.21 = (f32[5,1,8,896]{3,2,1,0:T(8,128)S(1)}, f32[5,1,8,896]{3,2,1,0:T(8,128)S(1)}, u32[]{:S(2)}, u32[]{:S(2)}) collective-permute-start(f32[5,1,8,896]{3,2,1,0:T(8,128)S(1)} %get-tuple-element.1993), channel_id=1, source_target_pairs={{2,0},{4,2},{6,4},{0,6},{3,1},{5,3},{7,5},{1,7},{10,8},{12,10},{14... | collective-permute-start | bytes 430088 | tf_op jit(solution)/shard_map/ppermute | solution.py:19
  150.0 1.4 collective-permute-start.22
  150.1 1.4 collective-permute-start.23
  (5 other events, 3.3 us)
where the time goes:
time: 153 us
  other arithmetic  88.9 us (58%)
  starting transfers between devices  30.6 us (20%)
  waiting for transfers between devices  25.6 us (17%)
  local copies, waits for them, and re-layouts  4.73 us (3%)
  loops' own time  2.33 us (2%)
    reduce_sum x9, other arithmetic, half_force_step(): jnp.sum(pair_force, axis=-2)  30.8 us
    ppermute x12, waiting for transfers between devices, padded_2(): before = lax.ppermute(last, axis, up)  20.8 us
    ppermute x12, starting transfers between devices, padded_2(): after = lax.ppermute(first, axis, down)  17.1 us
    reduce_sum x6, other arithmetic, half_force_step(): jnp.sum(energy_pair, axis=-2)[..., None, :]  14.6 us
    ppermute x12, starting transfers between devices, padded_2(): before = lax.ppermute(last, axis, up)  13.5 us
    reduce_sum x6, other arithmetic, separation(): return (displace, jnp.sum(displace * displace, axis=-3))  12 us
    mul x9, other arithmetic, half_force_step(): pair_force = 2.0 * coupling[..., None, :, :] * displace  10.3 us
    reduce_sum x6, other arithmetic, half_density_step(): jnp.sum(dens * plane_weight[..., :, None], axis=-2)  9.75 us
  transfers between devices with their start and end apart: 24, of which 21 were waited for; matrix products, arithmetic and copies ran while one was open for 0% of the time, Pallas kernels for 0%

commit v1 on v0

v1 whole, which is shorter than its diff:
```python
import math

import jax
import jax.numpy as jnp
from jax import lax
from jax.experimental import pallas as pl
from jax.experimental.pallas import tpu as pltpu
from jax.sharding import PartitionSpec as P

cut_square = 0.9025
density_rate = 3.0
lanes = 128

log2e = 1.0 / math.log(2.0)
unit = math.sqrt(density_rate * log2e)
reach = density_rate * log2e * cut_square
slope_offset = (2.0 / cut_square) * reach / 3.0
decay = 2.0 ** -reach
density_scale = decay / (reach * reach)
self_density = reach * reach / decay
self_energy = self_density / decay
energy_scale = 0.25 * decay * decay / (reach * reach)
force_scale = -6.0 * decay * decay / (reach * reach) / unit


def shifted(value, axis, step):
    peers = lax.axis_size(axis)
    if peers == 1:
        return value
    return lax.ppermute(value, axis, [(i, (i + step) % peers) for i in range(peers)])


def extend(value, axis, dim, width):
    length = value.shape[dim]
    last = lax.slice_in_dim(value, length - width, length, axis=dim)
    first = lax.slice_in_dim(value, 0, width, axis=dim)
    return jnp.concatenate([shifted(last, axis, 1), value, shifted(first, axis, -1)], axis=dim)


def z_peers(value):
    below = shifted(value, "gz", 1)
    above = below if lax.axis_size("gz") <= 2 else shifted(value, "gz", -1)
    return below, above


def lane_iota(rows):
    return lax.broadcasted_iota(jnp.int32, (rows, lanes), 1)


def same_cell(group):
    row = lax.broadcasted_iota(jnp.int32, (lanes, lanes), 0)
    col = lax.broadcasted_iota(jnp.int32, (lanes, lanes), 1)
    return jnp.where(row // group == col // group, 1.0, 0.0).astype(jnp.float32)


def windows(own, below, above, group):
    lane = lane_iota(own.shape[0])
    down = jnp.where(lane < group, pltpu.roll(below, group, 1), pltpu.roll(own, group, 1))
    up = jnp.where(
        lane >= lanes - group,
        pltpu.roll(above, lanes - group, 1),
        pltpu.roll(own, lanes - group, 1),
    )
    return down, own, up


def spread(rows, group, cell_sum):
    sub = lax.broadcasted_iota(jnp.int32, (group, lanes), 0)
    pick = (lane_iota(group) % group) == sub
    tall = jnp.concatenate(
        [jnp.where(pick, rows[r : r + 1], 0.0) for r in range(rows.shape[0])], axis=0
    )
    return jnp.dot(
        tall, cell_sum, precision=lax.Precision.HIGHEST, preferred_element_type=jnp.float32
    )


def gather_rows(tall, group):
    sub = lax.broadcasted_iota(jnp.int32, (group, lanes), 0)
    pick = (lane_iota(group) % group) == sub
    parts = tall.shape[0] // group
    return jnp.concatenate(
        [
            jnp.sum(jnp.where(pick, tall[p * group : (p + 1) * group], 0.0), axis=0, keepdims=True)
            for p in range(parts)
        ],
        axis=0,
    )


def fill_windows(own_ref, below_ref, above_ref, win_ref, first, size_x, size_y, parts, group):
    count = size_x * size_y

    def step(n, carry):
        x, y = n // size_y, n % size_y
        tiles = windows(
            own_ref[x + first, y + first],
            below_ref[x + first, y + first],
            above_ref[x + first, y + first],
            group,
        )
        row = lax.broadcasted_iota(jnp.int32, (4 * parts, lanes), 0)
        z_row = (row >= 2 * parts) & (row < 3 * parts)
        for k, tile in enumerate(tiles):
            win_ref[n * 3 + k] = tile + jnp.where(z_row, (k - 1) * unit, 0.0) if k != 1 else tile
        return carry

    lax.fori_loop(0, count, step, 0)


def density_kernel(own_ref, below_ref, above_ref, rows_ref, full_ref, win_ref, *, slots, group):
    wide_x, wide_y = own_ref.shape[0], own_ref.shape[1]
    parts = slots // group
    cell_sum = same_cell(group)
    fill_windows(own_ref, below_ref, above_ref, win_ref, 0, wide_x, wide_y, parts, group)
    inner_x, inner_y = wide_x - 2, wide_y - 2

    def column(n, carry):
        x, y = n // inner_y, n % inner_y
        rows = own_ref[x + 1, y + 1]
        own = spread(rows, group, cell_sum)
        px, py, pz, pw = [own[c * slots : (c + 1) * slots] for c in range(4)]

        def side(o, total):
            dx, dy = o // 3, o % 3
            base = ((x + dx) * wide_y + (y + dy)) * 3
            sx = (dx - 1).astype(jnp.float32) * unit
            sy = (dy - 1).astype(jnp.float32) * unit
            for k in range(3):
                tile = win_ref[base + k]
                for p in range(parts):
                    jx, jy, jz, jw = [tile[c * parts + p : c * parts + p + 1] for c in range(4)]
                    ax, ay, az = (jx + sx) - px, (jy + sy) - py, jz - pz
                    margin = jnp.maximum(reach - (ax * ax + ay * ay + az * az), 0.0)
                    total = total + (jnp.exp2(margin) * margin) * (margin * jw)
            return total

        total = lax.fori_loop(0, 9, side, jnp.zeros((slots, lanes), jnp.float32))
        total = jnp.dot(
            total, cell_sum, precision=lax.Precision.HIGHEST, preferred_element_type=jnp.float32
        )
        root = jnp.sqrt((total - self_density * pw) * density_scale + 1.0)
        full_ref[n] = root
        ratio = jnp.where(pw > 1.2, 1.4 / 1.6, jnp.where(pw > 0.0, 1.0, 0.0))
        rows_ref[n] = gather_rows(-ratio * (0.5 / decay) / root, group)
        return carry

    lax.fori_loop(0, inner_x * inner_y, column, 0)


def force_kernel(
    own_ref, below_ref, above_ref, root_ref, slope_ref, slope_below_ref, slope_above_ref,
    out_ref, win_ref, slope_win_ref, *, slots, group
):
    size_x, size_y, cells_z = out_ref.shape[0], out_ref.shape[1], out_ref.shape[2]
    wide_y = size_y + 2
    parts = slots // group
    cell_sum = same_cell(group)
    fill_windows(own_ref, below_ref, above_ref, win_ref, 1, size_x + 2, wide_y, parts, group)

    def slope_step(n, carry):
        tiles = windows(slope_ref[n], slope_below_ref[n], slope_above_ref[n], group)
        for k, tile in enumerate(tiles):
            slope_win_ref[n * 3 + k] = tile
        return carry

    lax.fori_loop(0, (size_x + 2) * wide_y, slope_step, 0)
    of_cell = jnp.where(
        lax.broadcasted_iota(jnp.int32, (cells_z, lanes), 1) // group
        == lax.broadcasted_iota(jnp.int32, (cells_z, lanes), 0),
        1.0,
        0.0,
    ).astype(jnp.float32)

    def column(n, carry):
        x, y = n // size_y, n % size_y
        here = (x + 1) * wide_y + y + 1
        own = spread(own_ref[x + 2, y + 2], group, cell_sum)
        px, py, pz, pw = [own[c * slots : (c + 1) * slots] for c in range(4)]
        root = root_ref[here]
        pt = -jnp.where(pw > 1.2, 1.4 / 1.6, jnp.where(pw > 0.0, 1.0, 0.0)) * (0.5 / decay) / root

        def side(o, sums):
            fx, fy, fz, en = sums
            dx, dy = o // 3, o % 3
            base = ((x + dx) * wide_y + (y + dy)) * 3
            sx = (dx - 1).astype(jnp.float32) * unit
            sy = (dy - 1).astype(jnp.float32) * unit
            for k in range(3):
                tile = win_ref[base + k]
                slope_tile = slope_win_ref[base + k]
                for p in range(parts):
                    jx, jy, jz, jw = [tile[c * parts + p : c * parts + p + 1] for c in range(4)]
                    jt = slope_tile[p : p + 1]
                    ax, ay, az = (jx + sx) - px, (jy + sy) - py, jz - pz
                    margin = jnp.maximum(reach - (ax * ax + ay * ay + az * az), 0.0)
                    power = jnp.exp2(margin)
                    edge = power * margin
                    weighted = edge * jw
                    v = weighted * (
                        (pt + jt) * (margin + slope_offset) + power * (margin + 0.5 * slope_offset)
                    )
                    fx, fy, fz = fx + v * ax, fy + v * ay, fz + v * az
                    en = en + weighted * edge
            return fx, fy, fz, en

        zero = jnp.zeros((slots, lanes), jnp.float32)
        fx, fy, fz, en = lax.fori_loop(0, 9, side, (zero, zero, zero, zero))
        embedding = jnp.where(pw > 1.2, 1.4, pw)
        scale = force_scale * pw
        energy = (en - (self_energy / group) * pw) * (energy_scale * pw) - embedding * root / group
        tall = jnp.concatenate([fx * scale, fy * scale, fz * scale, energy], axis=0)
        out_ref[x, y] = lax.dot_general(
            of_cell, tall, (((1,), (1,)), ((), ())),
            precision=lax.Precision.HIGHEST, preferred_element_type=jnp.float32,
        )
        return carry

    lax.fori_loop(0, size_x * size_y, column, 0)


def body(positions, types):
    size_x, size_y, cells_z, slots = types.shape
    group = lanes // cells_z
    parts = slots // group
    weight = jnp.where(types == 1, 1.0, jnp.where(types == 2, 1.6, 0.0)).astype(jnp.float32)
    value = jnp.concatenate([positions * unit, weight], axis=3)
    value = value.reshape(size_x, size_y, cells_z, 4 * parts, group)
    value = value.transpose(0, 1, 3, 2, 4).reshape(size_x, size_y, 4 * parts, lanes)
    value = extend(extend(value, "gx", 0, 2), "gy", 1, 2)
    below, above = z_peers(value)
    columns = (size_x + 2) * (size_y + 2)
    f32 = jnp.float32
    slope_rows, root = pl.pallas_call(
        lambda *refs: density_kernel(*refs, slots=slots, group=group),
        out_shape=(
            jax.ShapeDtypeStruct((columns, parts, lanes), f32),
            jax.ShapeDtypeStruct((columns, slots, lanes), f32),
        ),
        scratch_shapes=[
            pltpu.VMEM(((size_x + 4) * (size_y + 4) * 3, 4 * parts, lanes), f32)
        ],
        name="density",
    )(value, below, above)
    slope_below, slope_above = z_peers(slope_rows)
    return pl.pallas_call(
        lambda *refs: force_kernel(*refs, slots=slots, group=group),
        out_shape=jax.ShapeDtypeStruct((size_x, size_y, cells_z, 4 * slots), f32),
        scratch_shapes=[
            pltpu.VMEM((columns * 3, 4 * parts, lanes), f32),
            pltpu.VMEM((columns * 3, parts, lanes), f32),
        ],
        name="force",
    )(value, below, above, root, slope_rows, slope_below, slope_above)


def solution(mesh):
    in_specs = (P("gx", "gy", "gz", None), P("gx", "gy", "gz", None))
    out_specs = P("gx", "gy", "gz", None)
    return jax.shard_map(body, mesh=mesh, in_specs=in_specs, out_specs=out_specs, check_vma=False)
```

time: 153 us -> 71.6 us (0.47)
  other arithmetic: 88.9 us -> 0.88 us
  Pallas kernels: 0 us -> 52.5 us
  starting transfers between devices: 30.6 us -> 8.13 us
  waiting for transfers between devices: 25.6 us -> 7.96 us
  local copies, waits for them, and re-layouts: 4.73 us -> 1.91 us
  loops' own time: 2.33 us -> 0 us
    reduce_sum x27 -> x0, other arithmetic: 67.1 us -> none  [the longest x9 30.8 us: half_force_step(): jnp.sum(pair_force, axis=-2)]
    pallas_call x0 -> x2, Pallas kernels: none -> 52.5 us  [the longest x1 33.1 us: body(): pl.pallas_call(lambda *refs: density_kernel(*refs, slots=slots, group=gro...]
    ppermute x24 -> x6, starting transfers between devices: 30.6 us -> 8.13 us  [shifted(): lax.ppermute(value, axis, [(i, (i + step) % peers) for i in range(peers)])]
    ppermute x24 -> x6, waiting for transfers between devices: 25.6 us -> 7.96 us  [shifted(): lax.ppermute(value, axis, [(i, (i + step) % peers) for i in range(peers)])]
    mul x9 -> x1, other arithmetic: 10.3 us -> 0.78 us  [body(): value = jnp.concatenate([positions * unit, weight], axis=3)]
    dynamic_update_slice x93 -> x0, other arithmetic: 3.38 us -> none  [put_row(): return lax.dynamic_update_index_in_dim(array, value, index, 0)]
    slice x15 -> x0, other arithmetic: 3.16 us -> none  [the longest x9 2.76 us: padded_2(): last = lax.slice_in_dim(value, length - width, length, axis=dim)]
    another operation x2 -> x0, loops' own time: 2.33 us -> none  [the longest x1 1.39 us: body(): lax.fori_loop(0, cell_count_first, half_force_step, (force_start, pair_st...]
  transfers between devices with their start and end apart: 24 -> 6, of which waited for: 21 -> 6; matrix products, arithmetic and copies ran while one was open for 0% -> 0% of each run, Pallas kernels for 0% -> 0%
where the time goes in v1:
time: 71.6 us; the launch traced here: 71.4 us
  Pallas kernels  52.5 us (73%)
  starting transfers between devices  8.13 us (11%)
  waiting for transfers between devices  7.96 us (11%)
  local copies, waits for them, and re-layouts  1.91 us (3%)
  other arithmetic  0.88 us (1%)
    pallas_call x1, Pallas kernels, body(): pl.pallas_call(lambda *refs: density_kernel(*refs, slots=slots, group=gro...  33.1 us
    pallas_call x1, Pallas kernels, body(): pl.pallas_call(lambda *refs: force_kernel(*refs, slots=slots, group=group...  19.4 us
    ppermute x6, starting transfers between devices, shifted(): lax.ppermute(value, axis, [(i, (i + step) % peers) for i in range(peers)])  8.13 us
    ppermute x6, waiting for transfers between devices, shifted(): lax.ppermute(value, axis, [(i, (i + step) % peers) for i in range(peers)])  7.96 us
  transfers between devices with their start and end apart: 6, of which 6 were waited for; matrix products, arithmetic and copies ran while one was open for 0% of the time, Pallas kernels for 0%

profile of v1, /device:TPU:0, one launch (start us, length us, event | category | flops | bytes accessed | tf_op | source)
XLA Modules:
  0.0 71.4 jit_solution(10403053215422946948)
XLA Ops:
  0.0 0.0 copy-start.3
  0.0 0.8 %broadcast_multiply_fusion = f32[3,3,8,96]{3,2,1,0:T(8,128)S(1)} fusion(f32[3,3,8,96]{3,2,1,0:T(8,128)} %param.2), kind=kLoop, calls=%fused_computation.4 | loop fusion | flops 6912 | bytes 55296 | tf_op jit(solution)/shard_map/mul | solution.py:227
  0.8 0.0 copy-done.3
  0.8 0.1 pad_maximum_fusion.1
  0.9 0.1 reshape.8
  1.0 0.1 copy.5
  1.1 0.1 slice.19
  1.2 3.0 %collective-permute-start = (f32[2,3,8,128]{3,2,1,0:T(8,128)S(1)}, f32[2,3,8,128]{3,2,1,0:T(8,128)S(1)}, u32[]{:S(2)}, u32[]{:S(2)}) collective-permute-start(f32[2,3,8,128]{3,2,1,0:T(8,128)S(1)} %slice.19), channel_id=1, source_target_pairs={{0,8},{8,16},{16,24},{24,0},{1,9},{9,17},{17,25},{25,1},{2,10},{10... | collective-permute-start | bytes 73736 | tf_op jit(solution)/shard_map/ppermute | solution.py:30
  4.3 0.1 slice.21
  4.4 1.0 %collective-permute-start.1 = (f32[2,3,8,128]{3,2,1,0:T(8,128)S(1)}, f32[2,3,8,128]{3,2,1,0:T(8,128)S(1)}, u32[]{:S(2)}, u32[]{:S(2)}) collective-permute-start(f32[2,3,8,128]{3,2,1,0:T(8,128)S(1)} %slice.21), channel_id=1, source_target_pairs={{0,24},{8,0},{16,8},{24,16},{1,25},{9,1},{17,9},{25,17},{2,26},{10... | collective-permute-start | bytes 73736 | tf_op jit(solution)/shard_map/ppermute | solution.py:30
  5.4 0.1 reshape.9
  5.5 1.5 %collective-permute-done = f32[2,3,8,128]{3,2,1,0:T(8,128)S(1)} collective-permute-done((f32[2,3,8,128]{3,2,1,0:T(8,128)S(1)}, f32[2,3,8,128]{3,2,1,0:T(8,128)S(1)}, u32[]{:S(2)}, u32[]{:S(2)}) %collective-permute-start) | collective-permute-done | bytes 24608 | tf_op jit(solution)/shard_map/ppermute | solution.py:30
  7.0 1.2 %collective-permute-done.1 = f32[2,3,8,128]{3,2,1,0:T(8,128)S(1)} collective-permute-done((f32[2,3,8,128]{3,2,1,0:T(8,128)S(1)}, f32[2,3,8,128]{3,2,1,0:T(8,128)S(1)}, u32[]{:S(2)}, u32[]{:S(2)}) %collective-permute-start.1) | collective-permute-done | bytes 24608 | tf_op jit(solution)/shard_map/ppermute | solution.py:30
  8.3 1.6 %collective-permute-start.2 = (f32[7,2,8,128]{3,2,1,0:T(8,128)S(1)}, f32[7,2,8,128]{3,2,1,0:T(8,128)S(1)}, u32[]{:S(2)}, u32[]{:S(2)}) collective-permute-start(f32[7,2,8,128]{3,2,1,0:T(8,128)S(1)} %get-tuple-element.11), channel_id=1, source_target_pairs={{0,2},{2,4},{4,6},{6,0},{1,3},{3,5},{5,7},{7,1},{8,10},{10,12},{12... | collective-permute-start | bytes 172040 | tf_op jit(solution)/shard_map/ppermute | solution.py:30
  9.9 2.2 %collective-permute-start.3 = (f32[7,2,8,128]{3,2,1,0:T(8,128)S(1)}, f32[7,2,8,128]{3,2,1,0:T(8,128)S(1)}, u32[]{:S(2)}, u32[]{:S(2)}) collective-permute-start(f32[7,2,8,128]{3,2,1,0:T(8,128)S(1)} %get-tuple-element.12), channel_id=1, source_target_pairs={{0,6},{2,0},{4,2},{6,4},{1,7},{3,1},{5,3},{7,5},{8,14},{10,8},{12,... | collective-permute-start | bytes 172040 | tf_op jit(solution)/shard_map/ppermute | solution.py:30
  12.2 2.3 %collective-permute-done.2 = f32[7,2,8,128]{3,2,1,0:T(8,128)S(1)} collective-permute-done((f32[7,2,8,128]{3,2,1,0:T(8,128)S(1)}, f32[7,2,8,128]{3,2,1,0:T(8,128)S(1)}, u32[]{:S(2)}, u32[]{:S(2)}) %collective-permute-start.2) | collective-permute-done | bytes 57376 | tf_op jit(solution)/shard_map/ppermute | solution.py:30
  14.4 0.3 collective-permute-done.3
  14.7 0.0 copy-start.1
  14.7 0.1 collective-permute-start.4
  14.8 1.4 %collective-permute-done.4.refs_1_.refs_2_ = f32[7,7,8,128]{3,2,1,0:T(8,128)S(1)} collective-permute-done((f32[7,7,8,128]{3,2,1,0:T(8,128)S(1)}, f32[7,7,8,128]{3,2,1,0:T(8,128)S(1)}, u32[]{:S(2)}, u32[]{:S(2)}) %collective-permute-start.4) | collective-permute-done | bytes 200736 | tf_op jit(solution)/shard_map/ppermute | solution.py:30
  16.2 0.0 copy-done.1
  16.2 0.0 copy-start
  16.2 0.7 copy-done
  16.9 33.1 %density.1 = (f32[25,2,128]{2,1,0:T(2,128)}, f32[25,32,128]{2,1,0:T(8,128)}) custom-call(f32[7,7,8,128]{3,2,1,0:T(8,128)} %copy-done.1, f32[7,7,8,128]{3,2,1,0:T(8,128)} %copy-done, f32[7,7,8,128]{3,2,1,0:T(8,128)} %copy-done), custom_call_target="tpu_custom_call" | custom-call | tf_op jit(solution)/shard_map/density/pallas_call | solution.py:234
  50.0 0.1 collective-permute-start.5
  50.2 1.3 %collective-permute-done.5.refs_5_.refs_6_ = f32[25,2,128]{2,1,0:T(2,128)S(1)} collective-permute-done((f32[25,2,128]{2,1,0:T(2,128)}, f32[25,2,128]{2,1,0:T(2,128)S(1)}, u32[]{:S(2)}, u32[]{:S(2)}) %collective-permute-start.5) | collective-permute-done | bytes 25632 | tf_op jit(solution)/shard_map/ppermute | solution.py:30
  51.5 0.0 copy-start.2
  51.5 0.6 copy-done.2
  52.1 19.4 %force.1 = f32[3,3,8,128]{3,2,1,0:T(8,128)} custom-call(f32[7,7,8,128]{3,2,1,0:T(8,128)} %copy-done.1, f32[7,7,8,128]{3,2,1,0:T(8,128)} %copy-done, f32[7,7,8,128]{3,2,1,0:T(8,128)} %copy-done, f32[25,32,128]{2,1,0:T(8,128)} %get-tuple-element.7.refs_3_, f32[25,2,128]{2,1,0:T(2,128)} %get-tuple-element.8.refs_4_, f32[25,2,128]{2,1,0:T(2,128)} %copy-done.2, ...), custom_call_target="tpu_custom_call" | custom-call | tf_op jit(solution)/shard_map/force/pallas_call | solution.py:246
  (7 shorter events, 0.1 us)
Async XLA Ops:
  0.0 0.8 %copy-start.3 = (s32[3,3,8,32]{3,2,1,0:T(8,128)S(1)}, s32[3,3,8,32]{3,2,1,0:T(8,128)}, u32[]{:S(2)}) copy-start(s32[3,3,8,32]{3,2,1,0:T(8,128)} %param.3) | copy-start | bytes 27652
  1.2 5.8 %collective-permute-start = (f32[2,3,8,128]{3,2,1,0:T(8,128)S(1)}, f32[2,3,8,128]{3,2,1,0:T(8,128)S(1)}, u32[]{:S(2)}, u32[]{:S(2)}) collective-permute-start(f32[2,3,8,128]{3,2,1,0:T(8,128)S(1)} %slice.19), channel_id=1, source_target_pairs={{0,8},{8,16},{16,24},{24,0},{1,9},{9,17},{17,25},{25,1},{2,10},{10... | collective-permute-start | bytes 73736 | tf_op jit(solution)/shard_map/ppermute | solution.py:30
  4.4 3.9 %collective-permute-start.1 = (f32[2,3,8,128]{3,2,1,0:T(8,128)S(1)}, f32[2,3,8,128]{3,2,1,0:T(8,128)S(1)}, u32[]{:S(2)}, u32[]{:S(2)}) collective-permute-start(f32[2,3,8,128]{3,2,1,0:T(8,128)S(1)} %slice.21), channel_id=1, source_target_pairs={{0,24},{8,0},{16,8},{24,16},{1,25},{9,1},{17,9},{25,17},{2,26},{10... | collective-permute-start | bytes 73736 | tf_op jit(solution)/shard_map/ppermute | solution.py:30
  8.3 6.1 %collective-permute-start.2 = (f32[7,2,8,128]{3,2,1,0:T(8,128)S(1)}, f32[7,2,8,128]{3,2,1,0:T(8,128)S(1)}, u32[]{:S(2)}, u32[]{:S(2)}) collective-permute-start(f32[7,2,8,128]{3,2,1,0:T(8,128)S(1)} %get-tuple-element.11), channel_id=1, source_target_pairs={{0,2},{2,4},{4,6},{6,0},{1,3},{3,5},{5,7},{7,1},{8,10},{10,12},{12... | collective-permute-start | bytes 172040 | tf_op jit(solution)/shard_map/ppermute | solution.py:30
  9.9 4.8 %collective-permute-start.3 = (f32[7,2,8,128]{3,2,1,0:T(8,128)S(1)}, f32[7,2,8,128]{3,2,1,0:T(8,128)S(1)}, u32[]{:S(2)}, u32[]{:S(2)}) collective-permute-start(f32[7,2,8,128]{3,2,1,0:T(8,128)S(1)} %get-tuple-element.12), channel_id=1, source_target_pairs={{0,6},{2,0},{4,2},{6,4},{1,7},{3,1},{5,3},{7,5},{8,14},{10,8},{12,... | collective-permute-start | bytes 172040 | tf_op jit(solution)/shard_map/ppermute | solution.py:30
  14.7 1.5 %copy-start.1 = (f32[7,7,8,128]{3,2,1,0:T(8,128)}, f32[7,7,8,128]{3,2,1,0:T(8,128)S(1)}, u32[]{:S(2)}) copy-start(f32[7,7,8,128]{3,2,1,0:T(8,128)S(1)} %pad_maximum_fusion.refs_0_) | copy-start | bytes 602116
  14.7 1.5 %collective-permute-start.4 = (f32[7,7,8,128]{3,2,1,0:T(8,128)S(1)}, f32[7,7,8,128]{3,2,1,0:T(8,128)S(1)}, u32[]{:S(2)}, u32[]{:S(2)}) collective-permute-start(f32[7,7,8,128]{3,2,1,0:T(8,128)S(1)} %pad_maximum_fusion.refs_0_), channel_id=1, source_target_pairs={{0,1},{1,0},{2,3},{3,2},{4,5},{5,4},{6,7},{7,6},{8,9},{9,8},{10,11... | collective-permute-start | bytes 602120 | tf_op jit(solution)/shard_map/ppermute | solution.py:30
  16.2 0.7 copy-start
  50.0 1.4 %collective-permute-start.5 = (f32[25,2,128]{2,1,0:T(2,128)}, f32[25,2,128]{2,1,0:T(2,128)S(1)}, u32[]{:S(2)}, u32[]{:S(2)}) collective-permute-start(f32[25,2,128]{2,1,0:T(2,128)} %get-tuple-element.8.refs_4_), channel_id=1, source_target_pairs={{0,1},{1,0},{2,3},{3,2},{4,5},{5,4},{6,7},{7,6},{8,9},{9,8},{10,11... | collective-permute-start | bytes 76808 | tf_op jit(solution)/shard_map/ppermute | solution.py:30
  51.5 0.6 copy-start.2

commit v2 on v1

v2 whole, which is shorter than its diff:
```python
import math

import jax
import jax.numpy as jnp
from jax import lax
from jax.experimental import pallas as pl
from jax.experimental.pallas import tpu as pltpu
from jax.sharding import PartitionSpec as P

cut_square = 0.9025
density_rate = 3.0
lanes = 128

log2e = 1.0 / math.log(2.0)
unit = math.sqrt(density_rate * log2e)
reach = density_rate * log2e * cut_square
slope_offset = (2.0 / cut_square) * reach / 3.0
decay = 2.0 ** -reach
density_scale = decay / (reach * reach)
self_density = reach * reach / decay
self_energy = self_density / decay
energy_scale = 0.25 * decay * decay / (reach * reach)
force_scale = -6.0 * decay * decay / (reach * reach) / unit


def shifted(value, axis, step):
    peers = lax.axis_size(axis)
    if peers == 1:
        return value
    return lax.ppermute(value, axis, [(i, (i + step) % peers) for i in range(peers)])


def extend(value, axis, dim, width):
    length = value.shape[dim]
    last = lax.slice_in_dim(value, length - width, length, axis=dim)
    first = lax.slice_in_dim(value, 0, width, axis=dim)
    return jnp.concatenate([shifted(last, axis, 1), value, shifted(first, axis, -1)], axis=dim)


def z_peers(value):
    below = shifted(value, "gz", 1)
    above = below if lax.axis_size("gz") <= 2 else shifted(value, "gz", -1)
    return below, above


def lane_iota(rows):
    return lax.broadcasted_iota(jnp.int32, (rows, lanes), 1)


def same_cell(group):
    row = lax.broadcasted_iota(jnp.int32, (lanes, lanes), 0)
    col = lax.broadcasted_iota(jnp.int32, (lanes, lanes), 1)
    return jnp.where(row // group == col // group, 1.0, 0.0).astype(jnp.float32)


def windows(own, below, above, group):
    lane = lane_iota(own.shape[0])
    down = jnp.where(lane < group, pltpu.roll(below, group, 1), pltpu.roll(own, group, 1))
    up = jnp.where(
        lane >= lanes - group,
        pltpu.roll(above, lanes - group, 1),
        pltpu.roll(own, lanes - group, 1),
    )
    return down, own, up


def pieces(value):
    parts = []
    for _ in range(3):
        part = value.astype(jnp.bfloat16)
        parts.append(part)
        value = value - part.astype(jnp.float32)
    return parts


def exact_dot(value, ones, contract):
    ones = ones.astype(jnp.bfloat16)
    total = None
    for part in pieces(value):
        left, right = (ones, part) if contract == 1 else (part, ones)
        term = lax.dot_general(
            left, right, (((1,), (contract,)), ((), ())), preferred_element_type=jnp.float32
        )
        total = term if total is None else total + term
    return total


def pick_mask(group):
    sub = lax.broadcasted_iota(jnp.int32, (group, lanes), 0)
    return (lane_iota(group) % group) == sub


def spread(rows, group, cell_sum):
    pick = pick_mask(group)
    total = None
    ones = cell_sum.astype(jnp.bfloat16)
    for part in pieces(rows):
        part = part.astype(jnp.float32)
        tall = jnp.concatenate(
            [jnp.where(pick, part[r : r + 1], 0.0) for r in range(rows.shape[0])], axis=0
        ).astype(jnp.bfloat16)
        term = jnp.dot(tall, ones, preferred_element_type=jnp.float32)
        total = term if total is None else total + term
    return total


def gather_rows(tall, group):
    pick = pick_mask(group)
    parts = tall.shape[0] // group
    return jnp.concatenate(
        [
            jnp.sum(jnp.where(pick, tall[p * group : (p + 1) * group], 0.0), axis=0, keepdims=True)
            for p in range(parts)
        ],
        axis=0,
    )


def placed(rows, x, y, parts):
    row = lax.broadcasted_iota(jnp.int32, rows.shape, 0)
    along_x = jnp.where(row < parts, unit, 0.0)
    along_y = jnp.where((row >= parts) & (row < 2 * parts), unit, 0.0)
    at_x, at_y = jnp.asarray(x).astype(jnp.float32), jnp.asarray(y).astype(jnp.float32)
    return rows + (along_x * at_x + along_y * at_y)


def fill_windows(own_ref, below_ref, above_ref, win_ref, square_ref, first, count_x, count_y,
                 parts, group):
    center_x = 0.5 * (count_x - 1)
    center_y = 0.5 * (count_y - 1)
    row = lax.broadcasted_iota(jnp.int32, (4 * parts, lanes), 0)
    z_step = jnp.where((row >= 2 * parts) & (row < 3 * parts), unit, 0.0)

    def step(x, carry):
        for y in range(count_y):
            tiles = windows(
                own_ref[x + first, y + first],
                below_ref[x + first, y + first],
                above_ref[x + first, y + first],
                group,
            )
            for k, tile in enumerate(tiles):
                tile = placed(tile, x - center_x, y - center_y, parts) + (k - 1.0) * z_step
                n = (x * count_y + y) * 3 + k
                win_ref[n] = tile
                if square_ref is not None:
                    square = tile * tile
                    square_ref[n] = -(
                        square[:parts] + square[parts : 2 * parts] + square[2 * parts : 3 * parts]
                    )
        return carry

    lax.fori_loop(0, count_x, step, 0)


def type_ratio(weight):
    return jnp.where(weight > 1.2, 1.4 / 1.6, jnp.where(weight > 0.0, 1.0, 0.0))


def density_kernel(own_ref, below_ref, above_ref, rows_ref, root_ref, win_ref, square_ref,
                   full_ref, sum_ref, *, slots, group):
    wide_x, wide_y = own_ref.shape[0], own_ref.shape[1]
    parts = slots // group
    cell_sum = same_cell(group)
    fill_windows(own_ref, below_ref, above_ref, win_ref, square_ref, 0, wide_x, wide_y, parts,
                 group)
    inner_x, inner_y = wide_x - 2, wide_y - 2

    def spread_step(x, carry):
        for y in range(inner_y):
            rows = win_ref[((x + 1) * wide_y + y + 1) * 3 + 1]
            full_ref[x * inner_y + y] = spread(rows, group, cell_sum)
        return carry

    lax.fori_loop(0, inner_x, spread_step, 0)

    def column(n, carry):
        x, y = n // inner_y, n % inner_y
        px, py, pz = [full_ref[n, c * slots : (c + 1) * slots, :] for c in range(3)]
        room = reach - (px * px + py * py + pz * pz)
        px, py, pz = px + px, py + py, pz + pz

        def side(dx, total):
            base = ((x + dx) * wide_y + y) * 3
            for m in range(9):
                for p in range(parts):
                    jx, jy, jz, jw = [
                        win_ref[base + m, c * parts + p : c * parts + p + 1, :] for c in range(4)
                    ]
                    js = square_ref[base + m, p : p + 1, :]
                    margin = jnp.maximum((room + js) + px * jx + (py * jy + pz * jz), 0.0)
                    total = total + (jnp.exp2(margin) * margin) * (margin * jw)
            return total

        sum_ref[n] = lax.fori_loop(0, 3, side, jnp.zeros((slots, lanes), jnp.float32))
        return carry

    lax.fori_loop(0, inner_x * inner_y, column, 0)

    def finish(x, carry):
        for y in range(inner_y):
            n = x * inner_y + y
            pw = full_ref[n, 3 * slots : 4 * slots, :]
            total = exact_dot(sum_ref[n], cell_sum, 0)
            density = jnp.maximum(total - self_density * pw, 0.0) * density_scale
            root = jnp.sqrt(density + 1.0)
            root_ref[n] = root
            rows_ref[n] = gather_rows(-type_ratio(pw) * (0.5 / decay) / root, group)
        return carry

    lax.fori_loop(0, inner_x, finish, 0)


def force_kernel(
    own_ref, below_ref, above_ref, root_ref, slope_ref, slope_below_ref, slope_above_ref,
    out_ref, win_ref, slope_win_ref, full_ref, sum_ref, *, slots, group
):
    size_x, size_y, cells_z = out_ref.shape[0], out_ref.shape[1], out_ref.shape[2]
    wide_x, wide_y = size_x + 2, size_y + 2
    parts = slots // group
    cell_sum = same_cell(group)
    fill_windows(own_ref, below_ref, above_ref, win_ref, None, 1, wide_x, wide_y, parts, group)

    def slope_step(x, carry):
        for y in range(wide_y):
            n = x * wide_y + y
            tiles = windows(slope_ref[n], slope_below_ref[n], slope_above_ref[n], group)
            for k, tile in enumerate(tiles):
                slope_win_ref[n * 3 + k] = tile
        return carry

    lax.fori_loop(0, wide_x, slope_step, 0)
    of_cell = jnp.where(
        lane_iota(cells_z) // group == lax.broadcasted_iota(jnp.int32, (cells_z, lanes), 0),
        1.0,
        0.0,
    ).astype(jnp.float32)

    def spread_step(x, carry):
        for y in range(size_y):
            rows = win_ref[((x + 1) * wide_y + y + 1) * 3 + 1]
            full_ref[x * size_y + y] = spread(rows, group, cell_sum)
        return carry

    lax.fori_loop(0, size_x, spread_step, 0)
    half = slots // 2

    def column(n, carry):
        x, y = n // size_y, n % size_y
        here = (x + 1) * wide_y + y + 1
        for start in (0, half):
            px, py, pz, pw = [
                full_ref[n, c * slots + start : c * slots + start + half, :] for c in range(4)
            ]
            root = root_ref[here, start : start + half, :]
            pt = -type_ratio(pw) * (0.5 / decay) / root

            def side(dx, sums):
                fx, fy, fz, en = sums
                base = ((x + dx) * wide_y + y) * 3
                for m in range(9):
                    for p in range(parts):
                        jx, jy, jz, jw = [
                            win_ref[base + m, c * parts + p : c * parts + p + 1, :]
                            for c in range(4)
                        ]
                        jt = slope_win_ref[base + m, p : p + 1, :]
                        ax, ay, az = jx - px, jy - py, jz - pz
                        margin = jnp.maximum(reach - (ax * ax + ay * ay + az * az), 0.0)
                        power = jnp.exp2(margin)
                        edge = power * margin
                        weighted = edge * jw
                        v = weighted * (
                            (pt + jt) * (margin + slope_offset)
                            + power * (margin + 0.5 * slope_offset)
                        )
                        fx, fy, fz = fx + v * ax, fy + v * ay, fz + v * az
                        en = en + weighted * edge
                return fx, fy, fz, en

            zero = jnp.zeros((half, lanes), jnp.float32)
            fx, fy, fz, en = lax.fori_loop(0, 3, side, (zero, zero, zero, zero))
            embedding = jnp.where(pw > 1.2, 1.4, pw)
            scale = force_scale * pw
            sum_ref[n, start : start + half, :] = fx * scale
            sum_ref[n, slots + start : slots + start + half, :] = fy * scale
            sum_ref[n, 2 * slots + start : 2 * slots + start + half, :] = fz * scale
            sum_ref[n, 3 * slots + start : 3 * slots + start + half, :] = (
                en - (self_energy / group) * pw
            ) * (energy_scale * pw) - embedding * root * (1.0 / group)
        return carry

    lax.fori_loop(0, size_x * size_y, column, 0)

    def finish(x, carry):
        for y in range(size_y):
            out_ref[x, y] = exact_dot(sum_ref[x * size_y + y], of_cell, 1)
        return carry

    lax.fori_loop(0, size_x, finish, 0)


def body(positions, types):
    size_x, size_y, cells_z, slots = types.shape
    group = lanes // cells_z
    parts = slots // group
    weight = jnp.where(types == 1, 1.0, jnp.where(types == 2, 1.6, 0.0)).astype(jnp.float32)
    value = jnp.concatenate([positions * unit, weight], axis=3)
    value = value.reshape(size_x, size_y, cells_z, 4 * parts, group)
    value = value.transpose(0, 1, 3, 2, 4).reshape(size_x, size_y, 4 * parts, lanes)
    value = extend(extend(value, "gx", 0, 2), "gy", 1, 2)
    below, above = z_peers(value)
    columns = (size_x + 2) * (size_y + 2)
    f32 = jnp.float32
    slope_rows, root = pl.pallas_call(
        lambda *refs: density_kernel(*refs, slots=slots, group=group),
        out_shape=(
            jax.ShapeDtypeStruct((columns, parts, lanes), f32),
            jax.ShapeDtypeStruct((columns, slots, lanes), f32),
        ),
        scratch_shapes=[
            pltpu.VMEM(((size_x + 4) * (size_y + 4) * 3, 4 * parts, lanes), f32),
            pltpu.VMEM(((size_x + 4) * (size_y + 4) * 3, parts, lanes), f32),
            pltpu.VMEM((columns, 4 * slots, lanes), f32),
            pltpu.VMEM((columns, slots, lanes), f32),
        ],
        name="density",
    )(value, below, above)
    slope_below, slope_above = z_peers(slope_rows)
    return pl.pallas_call(
        lambda *refs: force_kernel(*refs, slots=slots, group=group),
        out_shape=jax.ShapeDtypeStruct((size_x, size_y, cells_z, 4 * slots), f32),
        scratch_shapes=[
            pltpu.VMEM((columns * 3, 4 * parts, lanes), f32),
            pltpu.VMEM((columns * 3, parts, lanes), f32),
            pltpu.VMEM((size_x * size_y, 4 * slots, lanes), f32),
            pltpu.VMEM((size_x * size_y, 4 * slots, lanes), f32),
        ],
        name="force",
    )(value, below, above, root, slope_rows, slope_below, slope_above)


def solution(mesh):
    in_specs = (P("gx", "gy", "gz", None), P("gx", "gy", "gz", None))
    out_specs = P("gx", "gy", "gz", None)
    return jax.shard_map(body, mesh=mesh, in_specs=in_specs, out_specs=out_specs, check_vma=False)
```

time: 71.6 us -> 47 us (0.66)
  Pallas kernels: 52.5 us -> 27.9 us
    pallas_call x1, Pallas kernels: 33.1 us -> 15.7 us  [body(): pl.pallas_call(lambda *refs: density_kernel(*refs, slots=slots, group=gro...]
    pallas_call x1, Pallas kernels: 19.4 us -> 12.2 us  [body(): pl.pallas_call(lambda *refs: force_kernel(*refs, slots=slots, group=group...]
  transfers between devices with their start and end apart: 6 -> 6, of which waited for: 6 -> 6; matrix products, arithmetic and copies ran while one was open for 0% -> 1% of each run, Pallas kernels for 0% -> 0%
where the time goes in v2:
time: 47 us; the launch traced here: 46.8 us
  Pallas kernels  27.9 us (59%)
  starting transfers between devices  8.11 us (17%)
  waiting for transfers between devices  7.97 us (17%)
  local copies, waits for them, and re-layouts  1.91 us (4%)
  other arithmetic  0.88 us (2%)
    pallas_call x1, Pallas kernels, body(): pl.pallas_call(lambda *refs: density_kernel(*refs, slots=slots, group=gro...  15.7 us
    pallas_call x1, Pallas kernels, body(): pl.pallas_call(lambda *refs: force_kernel(*refs, slots=slots, group=group...  12.2 us
    ppermute x6, starting transfers between devices, shifted(): lax.ppermute(value, axis, [(i, (i + step) % peers) for i in range(peers)])  8.11 us
    ppermute x6, waiting for transfers between devices, shifted(): lax.ppermute(value, axis, [(i, (i + step) % peers) for i in range(peers)])  7.97 us
    unnamed x10, local copies, waits for them, and re-layouts  1.32 us
  transfers between devices with their start and end apart: 6, of which 6 were waited for; matrix products, arithmetic and copies ran while one was open for 1% of the time, Pallas kernels for 0%

profile of v2, /device:TPU:0, one launch (start us, length us, event | category | flops | bytes accessed | tf_op | source)
XLA Modules:
  0.0 46.8 jit_solution(1112929959072276416)
XLA Ops:
  0.0 0.0 copy-start.3
  0.0 0.8 %broadcast_multiply_fusion = f32[3,3,8,96]{3,2,1,0:T(8,128)S(1)} fusion(f32[3,3,8,96]{3,2,1,0:T(8,128)} %param.2), kind=kLoop, calls=%fused_computation.4 | loop fusion | flops 6912 | bytes 55296 | tf_op jit(solution)/shard_map/mul | solution.py:308
  0.8 0.0 copy-done.3
  0.8 0.1 pad_maximum_fusion.1
  0.9 0.1 reshape.8
  1.0 0.1 copy.5
  1.1 0.1 slice.19
  1.2 3.0 %collective-permute-start = (f32[2,3,8,128]{3,2,1,0:T(8,128)S(1)}, f32[2,3,8,128]{3,2,1,0:T(8,128)S(1)}, u32[]{:S(2)}, u32[]{:S(2)}) collective-permute-start(f32[2,3,8,128]{3,2,1,0:T(8,128)S(1)} %slice.19), channel_id=1, source_target_pairs={{0,8},{8,16},{16,24},{24,0},{1,9},{9,17},{17,25},{25,1},{2,10},{10... | collective-permute-start | bytes 73736 | tf_op jit(solution)/shard_map/ppermute | solution.py:30
  4.3 0.1 slice.21
  4.4 1.0 %collective-permute-start.1 = (f32[2,3,8,128]{3,2,1,0:T(8,128)S(1)}, f32[2,3,8,128]{3,2,1,0:T(8,128)S(1)}, u32[]{:S(2)}, u32[]{:S(2)}) collective-permute-start(f32[2,3,8,128]{3,2,1,0:T(8,128)S(1)} %slice.21), channel_id=1, source_target_pairs={{0,24},{8,0},{16,8},{24,16},{1,25},{9,1},{17,9},{25,17},{2,26},{10... | collective-permute-start | bytes 73736 | tf_op jit(solution)/shard_map/ppermute | solution.py:30
  5.4 0.1 reshape.9
  5.5 1.5 %collective-permute-done = f32[2,3,8,128]{3,2,1,0:T(8,128)S(1)} collective-permute-done((f32[2,3,8,128]{3,2,1,0:T(8,128)S(1)}, f32[2,3,8,128]{3,2,1,0:T(8,128)S(1)}, u32[]{:S(2)}, u32[]{:S(2)}) %collective-permute-start) | collective-permute-done | bytes 24608 | tf_op jit(solution)/shard_map/ppermute | solution.py:30
  7.0 1.2 %collective-permute-done.1 = f32[2,3,8,128]{3,2,1,0:T(8,128)S(1)} collective-permute-done((f32[2,3,8,128]{3,2,1,0:T(8,128)S(1)}, f32[2,3,8,128]{3,2,1,0:T(8,128)S(1)}, u32[]{:S(2)}, u32[]{:S(2)}) %collective-permute-start.1) | collective-permute-done | bytes 24608 | tf_op jit(solution)/shard_map/ppermute | solution.py:30
  8.3 1.6 %collective-permute-start.2 = (f32[7,2,8,128]{3,2,1,0:T(8,128)S(1)}, f32[7,2,8,128]{3,2,1,0:T(8,128)S(1)}, u32[]{:S(2)}, u32[]{:S(2)}) collective-permute-start(f32[7,2,8,128]{3,2,1,0:T(8,128)S(1)} %get-tuple-element.11), channel_id=1, source_target_pairs={{0,2},{2,4},{4,6},{6,0},{1,3},{3,5},{5,7},{7,1},{8,10},{10,12},{12... | collective-permute-start | bytes 172040 | tf_op jit(solution)/shard_map/ppermute | solution.py:30
  9.9 2.2 %collective-permute-start.3 = (f32[7,2,8,128]{3,2,1,0:T(8,128)S(1)}, f32[7,2,8,128]{3,2,1,0:T(8,128)S(1)}, u32[]{:S(2)}, u32[]{:S(2)}) collective-permute-start(f32[7,2,8,128]{3,2,1,0:T(8,128)S(1)} %get-tuple-element.12), channel_id=1, source_target_pairs={{0,6},{2,0},{4,2},{6,4},{1,7},{3,1},{5,3},{7,5},{8,14},{10,8},{12,... | collective-permute-start | bytes 172040 | tf_op jit(solution)/shard_map/ppermute | solution.py:30
  12.2 2.3 %collective-permute-done.2 = f32[7,2,8,128]{3,2,1,0:T(8,128)S(1)} collective-permute-done((f32[7,2,8,128]{3,2,1,0:T(8,128)S(1)}, f32[7,2,8,128]{3,2,1,0:T(8,128)S(1)}, u32[]{:S(2)}, u32[]{:S(2)}) %collective-permute-start.2) | collective-permute-done | bytes 57376 | tf_op jit(solution)/shard_map/ppermute | solution.py:30
  14.4 0.3 collective-permute-done.3
  14.7 0.0 copy-start.1
  14.7 0.1 collective-permute-start.4
  14.8 1.4 %collective-permute-done.4.refs_1_.refs_2_ = f32[7,7,8,128]{3,2,1,0:T(8,128)S(1)} collective-permute-done((f32[7,7,8,128]{3,2,1,0:T(8,128)S(1)}, f32[7,7,8,128]{3,2,1,0:T(8,128)S(1)}, u32[]{:S(2)}, u32[]{:S(2)}) %collective-permute-start.4) | collective-permute-done | bytes 200736 | tf_op jit(solution)/shard_map/ppermute | solution.py:30
  16.2 0.0 copy-done.1
  16.2 0.0 copy-start
  16.2 0.7 %copy-done = f32[7,7,8,128]{3,2,1,0:T(8,128)} copy-done((f32[7,7,8,128]{3,2,1,0:T(8,128)}, f32[7,7,8,128]{3,2,1,0:T(8,128)S(1)}, u32[]{:S(2)}) %copy-start) | copy-done | bytes 200728
  16.9 15.7 %density.1 = (f32[25,2,128]{2,1,0:T(2,128)}, f32[25,32,128]{2,1,0:T(8,128)}) custom-call(f32[7,7,8,128]{3,2,1,0:T(8,128)} %copy-done.1, f32[7,7,8,128]{3,2,1,0:T(8,128)} %copy-done, f32[7,7,8,128]{3,2,1,0:T(8,128)} %copy-done), custom_call_target="tpu_custom_call" | custom-call | tf_op jit(solution)/shard_map/density/pallas_call | solution.py:315
  32.6 0.1 collective-permute-start.5
  32.8 1.3 %collective-permute-done.5.refs_5_.refs_6_ = f32[25,2,128]{2,1,0:T(2,128)S(1)} collective-permute-done((f32[25,2,128]{2,1,0:T(2,128)}, f32[25,2,128]{2,1,0:T(2,128)S(1)}, u32[]{:S(2)}, u32[]{:S(2)}) %collective-permute-start.5) | collective-permute-done | bytes 25632 | tf_op jit(solution)/shard_map/ppermute | solution.py:30
  34.0 0.0 copy-start.2
  34.0 0.6 %copy-done.2 = f32[25,2,128]{2,1,0:T(2,128)} copy-done((f32[25,2,128]{2,1,0:T(2,128)}, f32[25,2,128]{2,1,0:T(2,128)S(1)}, u32[]{:S(2)}) %copy-start.2) | copy-done | bytes 25624
  34.7 12.2 %force.1 = f32[3,3,8,128]{3,2,1,0:T(8,128)} custom-call(f32[7,7,8,128]{3,2,1,0:T(8,128)} %copy-done.1, f32[7,7,8,128]{3,2,1,0:T(8,128)} %copy-done, f32[7,7,8,128]{3,2,1,0:T(8,128)} %copy-done, f32[25,32,128]{2,1,0:T(8,128)} %get-tuple-element.7.refs_3_, f32[25,2,128]{2,1,0:T(2,128)} %get-tuple-element.8.refs_4_, f32[25,2,128]{2,1,0:T(2,128)} %copy-done.2, ...), custom_call_target="tpu_custom_call" | custom-call | tf_op jit(solution)/shard_map/force/pallas_call | solution.py:330
  (7 shorter events, 0.1 us)
Async XLA Ops:
  0.0 0.8 %copy-start.3 = (s32[3,3,8,32]{3,2,1,0:T(8,128)S(1)}, s32[3,3,8,32]{3,2,1,0:T(8,128)}, u32[]{:S(2)}) copy-start(s32[3,3,8,32]{3,2,1,0:T(8,128)} %param.3) | copy-start | bytes 27652
  1.2 5.8 %collective-permute-start = (f32[2,3,8,128]{3,2,1,0:T(8,128)S(1)}, f32[2,3,8,128]{3,2,1,0:T(8,128)S(1)}, u32[]{:S(2)}, u32[]{:S(2)}) collective-permute-start(f32[2,3,8,128]{3,2,1,0:T(8,128)S(1)} %slice.19), channel_id=1, source_target_pairs={{0,8},{8,16},{16,24},{24,0},{1,9},{9,17},{17,25},{25,1},{2,10},{10... | collective-permute-start | bytes 73736 | tf_op jit(solution)/shard_map/ppermute | solution.py:30
  4.4 3.9 %collective-permute-start.1 = (f32[2,3,8,128]{3,2,1,0:T(8,128)S(1)}, f32[2,3,8,128]{3,2,1,0:T(8,128)S(1)}, u32[]{:S(2)}, u32[]{:S(2)}) collective-permute-start(f32[2,3,8,128]{3,2,1,0:T(8,128)S(1)} %slice.21), channel_id=1, source_target_pairs={{0,24},{8,0},{16,8},{24,16},{1,25},{9,1},{17,9},{25,17},{2,26},{10... | collective-permute-start | bytes 73736 | tf_op jit(solution)/shard_map/ppermute | solution.py:30
  8.3 6.1 %collective-permute-start.2 = (f32[7,2,8,128]{3,2,1,0:T(8,128)S(1)}, f32[7,2,8,128]{3,2,1,0:T(8,128)S(1)}, u32[]{:S(2)}, u32[]{:S(2)}) collective-permute-start(f32[7,2,8,128]{3,2,1,0:T(8,128)S(1)} %get-tuple-element.11), channel_id=1, source_target_pairs={{0,2},{2,4},{4,6},{6,0},{1,3},{3,5},{5,7},{7,1},{8,10},{10,12},{12... | collective-permute-start | bytes 172040 | tf_op jit(solution)/shard_map/ppermute | solution.py:30
  9.9 4.8 %collective-permute-start.3 = (f32[7,2,8,128]{3,2,1,0:T(8,128)S(1)}, f32[7,2,8,128]{3,2,1,0:T(8,128)S(1)}, u32[]{:S(2)}, u32[]{:S(2)}) collective-permute-start(f32[7,2,8,128]{3,2,1,0:T(8,128)S(1)} %get-tuple-element.12), channel_id=1, source_target_pairs={{0,6},{2,0},{4,2},{6,4},{1,7},{3,1},{5,3},{7,5},{8,14},{10,8},{12,... | collective-permute-start | bytes 172040 | tf_op jit(solution)/shard_map/ppermute | solution.py:30
  14.7 1.5 %copy-start.1 = (f32[7,7,8,128]{3,2,1,0:T(8,128)}, f32[7,7,8,128]{3,2,1,0:T(8,128)S(1)}, u32[]{:S(2)}) copy-start(f32[7,7,8,128]{3,2,1,0:T(8,128)S(1)} %pad_maximum_fusion.refs_0_) | copy-start | bytes 602116
  14.7 1.5 %collective-permute-start.4 = (f32[7,7,8,128]{3,2,1,0:T(8,128)S(1)}, f32[7,7,8,128]{3,2,1,0:T(8,128)S(1)}, u32[]{:S(2)}, u32[]{:S(2)}) collective-permute-start(f32[7,7,8,128]{3,2,1,0:T(8,128)S(1)} %pad_maximum_fusion.refs_0_), channel_id=1, source_target_pairs={{0,1},{1,0},{2,3},{3,2},{4,5},{5,4},{6,7},{7,6},{8,9},{9,8},{10,11... | collective-permute-start | bytes 602120 | tf_op jit(solution)/shard_map/ppermute | solution.py:30
  16.2 0.7 %copy-start = (f32[7,7,8,128]{3,2,1,0:T(8,128)}, f32[7,7,8,128]{3,2,1,0:T(8,128)S(1)}, u32[]{:S(2)}) copy-start(f32[7,7,8,128]{3,2,1,0:T(8,128)S(1)} %collective-permute-done.4.refs_1_.refs_2_) | copy-start | bytes 602116
  32.6 1.4 %collective-permute-start.5 = (f32[25,2,128]{2,1,0:T(2,128)}, f32[25,2,128]{2,1,0:T(2,128)S(1)}, u32[]{:S(2)}, u32[]{:S(2)}) collective-permute-start(f32[25,2,128]{2,1,0:T(2,128)} %get-tuple-element.8.refs_4_), channel_id=1, source_target_pairs={{0,1},{1,0},{2,3},{3,2},{4,5},{5,4},{6,7},{7,6},{8,9},{9,8},{10,11... | collective-permute-start | bytes 76808 | tf_op jit(solution)/shard_map/ppermute | solution.py:30
  34.0 0.6 %copy-start.2 = (f32[25,2,128]{2,1,0:T(2,128)}, f32[25,2,128]{2,1,0:T(2,128)S(1)}, u32[]{:S(2)}) copy-start(f32[25,2,128]{2,1,0:T(2,128)S(1)} %collective-permute-done.5.refs_5_.refs_6_) | copy-start | bytes 76804

commit v3 on v2

--- a/solution.py
+++ b/solution.py
@@ -157,8 +157,8 @@
     return jnp.where(weight > 1.2, 1.4 / 1.6, jnp.where(weight > 0.0, 1.0, 0.0))
 
 
-def density_kernel(own_ref, below_ref, above_ref, rows_ref, root_ref, win_ref, square_ref,
-                   full_ref, sum_ref, *, slots, group):
+def density_kernel(own_ref, below_ref, above_ref, rows_ref, win_ref, square_ref, full_ref,
+                   sum_ref, *, slots, group):
     wide_x, wide_y = own_ref.shape[0], own_ref.shape[1]
     parts = slots // group
     cell_sum = same_cell(group)
@@ -180,7 +180,8 @@
         room = reach - (px * px + py * py + pz * pz)
         px, py, pz = px + px, py + py, pz + pz
 
-        def side(dx, total):
+        total = jnp.zeros((slots, lanes), jnp.float32)
+        for dx in range(3):
             base = ((x + dx) * wide_y + y) * 3
             for m in range(9):
                 for p in range(parts):
@@ -190,9 +191,7 @@
                     js = square_ref[base + m, p : p + 1, :]
                     margin = jnp.maximum((room + js) + px * jx + (py * jy + pz * jz), 0.0)
                     total = total + (jnp.exp2(margin) * margin) * (margin * jw)
-            return total
-
-        sum_ref[n] = lax.fori_loop(0, 3, side, jnp.zeros((slots, lanes), jnp.float32))
+        sum_ref[n] = total
         return carry
 
     lax.fori_loop(0, inner_x * inner_y, column, 0)
@@ -203,16 +202,14 @@
             pw = full_ref[n, 3 * slots : 4 * slots, :]
             total = exact_dot(sum_ref[n], cell_sum, 0)
             density = jnp.maximum(total - self_density * pw, 0.0) * density_scale
-            root = jnp.sqrt(density + 1.0)
-            root_ref[n] = root
-            rows_ref[n] = gather_rows(-type_ratio(pw) * (0.5 / decay) / root, group)
+            rows_ref[n] = gather_rows(jnp.sqrt(density + 1.0), group)
         return carry
 
     lax.fori_loop(0, inner_x, finish, 0)
 
 
 def force_kernel(
-    own_ref, below_ref, above_ref, root_ref, slope_ref, slope_below_ref, slope_above_ref,
+    own_ref, below_ref, above_ref, rows_ref, rows_below_ref, rows_above_ref,
     out_ref, win_ref, slope_win_ref, full_ref, sum_ref, *, slots, group
 ):
     size_x, size_y, cells_z = out_ref.shape[0], out_ref.shape[1], out_ref.shape[2]
@@ -224,9 +221,10 @@
     def slope_step(x, carry):
         for y in range(wide_y):
             n = x * wide_y + y
-            tiles = windows(slope_ref[n], slope_below_ref[n], slope_above_ref[n], group)
+            tiles = windows(rows_ref[n], rows_below_ref[n], rows_above_ref[n], group)
             for k, tile in enumerate(tiles):
-                slope_win_ref[n * 3 + k] = tile
+                weight = win_ref[n * 3 + k, 3 * parts : 4 * parts, :]
+                slope_win_ref[n * 3 + k] = -type_ratio(weight) * (0.5 / decay) / tile
         return carry
 
     lax.fori_loop(0, wide_x, slope_step, 0)
@@ -239,6 +237,7 @@
     def spread_step(x, carry):
         for y in range(size_y):
             rows = win_ref[((x + 1) * wide_y + y + 1) * 3 + 1]
+            rows = jnp.concatenate([rows, rows_ref[(x + 1) * wide_y + y + 1]], axis=0)
             full_ref[x * size_y + y] = spread(rows, group, cell_sum)
         return carry
 
@@ -247,12 +246,10 @@
 
     def column(n, carry):
         x, y = n // size_y, n % size_y
-        here = (x + 1) * wide_y + y + 1
         for start in (0, half):
-            px, py, pz, pw = [
-                full_ref[n, c * slots + start : c * slots + start + half, :] for c in range(4)
+            px, py, pz, pw, root = [
+                full_ref[n, c * slots + start : c * slots + start + half, :] for c in range(5)
             ]
-            root = root_ref[here, start : start + half, :]
             pt = -type_ratio(pw) * (0.5 / decay) / root
 
             def side(dx, sums):
@@ -312,12 +309,9 @@
     below, above = z_peers(value)
     columns = (size_x + 2) * (size_y + 2)
     f32 = jnp.float32
-    slope_rows, root = pl.pallas_call(
+    root_rows = pl.pallas_call(
         lambda *refs: density_kernel(*refs, slots=slots, group=group),
-        out_shape=(
-            jax.ShapeDtypeStruct((columns, parts, lanes), f32),
-            jax.ShapeDtypeStruct((columns, slots, lanes), f32),
-        ),
+        out_shape=jax.ShapeDtypeStruct((columns, parts, lanes), f32),
         scratch_shapes=[
             pltpu.VMEM(((size_x + 4) * (size_y + 4) * 3, 4 * parts, lanes), f32),
             pltpu.VMEM(((size_x + 4) * (size_y + 4) * 3, parts, lanes), f32),
@@ -326,18 +320,18 @@
         ],
         name="density",
     )(value, below, above)
-    slope_below, slope_above = z_peers(slope_rows)
+    root_below, root_above = z_peers(root_rows)
     return pl.pallas_call(
         lambda *refs: force_kernel(*refs, slots=slots, group=group),
         out_shape=jax.ShapeDtypeStruct((size_x, size_y, cells_z, 4 * slots), f32),
         scratch_shapes=[
             pltpu.VMEM((columns * 3, 4 * parts, lanes), f32),
             pltpu.VMEM((columns * 3, parts, lanes), f32),
-            pltpu.VMEM((size_x * size_y, 4 * slots, lanes), f32),
+            pltpu.VMEM((size_x * size_y, 5 * slots, lanes), f32),
             pltpu.VMEM((size_x * size_y, 4 * slots, lanes), f32),
         ],
         name="force",
-    )(value, below, above, root, slope_rows, slope_below, slope_above)
+    )(value, below, above, root_rows, root_below, root_above)
 
 
 def solution(mesh):

time: 47 us -> 46.4 us (0.987)
  Pallas kernels: 27.9 us -> 27.2 us
    pallas_call x1, Pallas kernels: 15.7 us -> 15.1 us  [body(): pl.pallas_call(lambda *refs: density_kernel(*refs, slots=slots, group=gro...]
where the time goes in v3:
time: 46.4 us; the launch traced here: 46.2 us
  Pallas kernels  27.2 us (59%)
  starting transfers between devices  8.13 us (18%)
  waiting for transfers between devices  7.95 us (17%)
  local copies, waits for them, and re-layouts  1.88 us (4%)
  other arithmetic  0.88 us (2%)
    pallas_call x1, Pallas kernels, body(): pl.pallas_call(lambda *refs: density_kernel(*refs, slots=slots, group=gro...  15.1 us
    pallas_call x1, Pallas kernels, body(): pl.pallas_call(lambda *refs: force_kernel(*refs, slots=slots, group=group...  12.1 us
    ppermute x6, starting transfers between devices, shifted(): lax.ppermute(value, axis, [(i, (i + step) % peers) for i in range(peers)])  8.13 us
    ppermute x6, waiting for transfers between devices, shifted(): lax.ppermute(value, axis, [(i, (i + step) % peers) for i in range(peers)])  7.95 us
    unnamed x10, local copies, waits for them, and re-layouts  1.3 us
  transfers between devices with their start and end apart: 6, of which 6 were waited for; matrix products, arithmetic and copies ran while one was open for 1% of the time, Pallas kernels for 0%

profile of v3, /device:TPU:0, one launch (start us, length us, event | category | flops | bytes accessed | tf_op | source)
XLA Modules:
  0.0 46.2 jit_solution(15412784089055043220)
XLA Ops:
  0.0 0.0 copy-start.3
  0.0 0.8 %broadcast_multiply_fusion = f32[3,3,8,96]{3,2,1,0:T(8,128)S(1)} fusion(f32[3,3,8,96]{3,2,1,0:T(8,128)} %param.2), kind=kLoop, calls=%fused_computation.4 | loop fusion | flops 6912 | bytes 55296 | tf_op jit(solution)/shard_map/mul | solution.py:305
  0.8 0.0 copy-done.3
  0.8 0.1 pad_maximum_fusion.1
  0.9 0.1 reshape.8
  1.0 0.1 copy.5
  1.1 0.1 slice.19
  1.2 3.0 %collective-permute-start = (f32[2,3,8,128]{3,2,1,0:T(8,128)S(1)}, f32[2,3,8,128]{3,2,1,0:T(8,128)S(1)}, u32[]{:S(2)}, u32[]{:S(2)}) collective-permute-start(f32[2,3,8,128]{3,2,1,0:T(8,128)S(1)} %slice.19), channel_id=1, source_target_pairs={{0,8},{8,16},{16,24},{24,0},{1,9},{9,17},{17,25},{25,1},{2,10},{10... | collective-permute-start | bytes 73736 | tf_op jit(solution)/shard_map/ppermute | solution.py:30
  4.3 0.1 slice.21
  4.4 1.0 %collective-permute-start.1 = (f32[2,3,8,128]{3,2,1,0:T(8,128)S(1)}, f32[2,3,8,128]{3,2,1,0:T(8,128)S(1)}, u32[]{:S(2)}, u32[]{:S(2)}) collective-permute-start(f32[2,3,8,128]{3,2,1,0:T(8,128)S(1)} %slice.21), channel_id=1, source_target_pairs={{0,24},{8,0},{16,8},{24,16},{1,25},{9,1},{17,9},{25,17},{2,26},{10... | collective-permute-start | bytes 73736 | tf_op jit(solution)/shard_map/ppermute | solution.py:30
  5.4 0.1 reshape.9
  5.5 1.5 %collective-permute-done = f32[2,3,8,128]{3,2,1,0:T(8,128)S(1)} collective-permute-done((f32[2,3,8,128]{3,2,1,0:T(8,128)S(1)}, f32[2,3,8,128]{3,2,1,0:T(8,128)S(1)}, u32[]{:S(2)}, u32[]{:S(2)}) %collective-permute-start) | collective-permute-done | bytes 24608 | tf_op jit(solution)/shard_map/ppermute | solution.py:30
  7.0 1.2 %collective-permute-done.1 = f32[2,3,8,128]{3,2,1,0:T(8,128)S(1)} collective-permute-done((f32[2,3,8,128]{3,2,1,0:T(8,128)S(1)}, f32[2,3,8,128]{3,2,1,0:T(8,128)S(1)}, u32[]{:S(2)}, u32[]{:S(2)}) %collective-permute-start.1) | collective-permute-done | bytes 24608 | tf_op jit(solution)/shard_map/ppermute | solution.py:30
  8.3 1.6 %collective-permute-start.2 = (f32[7,2,8,128]{3,2,1,0:T(8,128)S(1)}, f32[7,2,8,128]{3,2,1,0:T(8,128)S(1)}, u32[]{:S(2)}, u32[]{:S(2)}) collective-permute-start(f32[7,2,8,128]{3,2,1,0:T(8,128)S(1)} %get-tuple-element.7), channel_id=1, source_target_pairs={{0,2},{2,4},{4,6},{6,0},{1,3},{3,5},{5,7},{7,1},{8,10},{10,12},{12... | collective-permute-start | bytes 172040 | tf_op jit(solution)/shard_map/ppermute | solution.py:30
  9.9 2.2 %collective-permute-start.3 = (f32[7,2,8,128]{3,2,1,0:T(8,128)S(1)}, f32[7,2,8,128]{3,2,1,0:T(8,128)S(1)}, u32[]{:S(2)}, u32[]{:S(2)}) collective-permute-start(f32[7,2,8,128]{3,2,1,0:T(8,128)S(1)} %get-tuple-element.8), channel_id=1, source_target_pairs={{0,6},{2,0},{4,2},{6,4},{1,7},{3,1},{5,3},{7,5},{8,14},{10,8},{12,... | collective-permute-start | bytes 172040 | tf_op jit(solution)/shard_map/ppermute | solution.py:30
  12.2 2.3 %collective-permute-done.2 = f32[7,2,8,128]{3,2,1,0:T(8,128)S(1)} collective-permute-done((f32[7,2,8,128]{3,2,1,0:T(8,128)S(1)}, f32[7,2,8,128]{3,2,1,0:T(8,128)S(1)}, u32[]{:S(2)}, u32[]{:S(2)}) %collective-permute-start.2) | collective-permute-done | bytes 57376 | tf_op jit(solution)/shard_map/ppermute | solution.py:30
  14.4 0.3 collective-permute-done.3
  14.7 0.0 copy-start.1
  14.7 0.1 collective-permute-start.4
  14.8 1.4 %collective-permute-done.4.refs_1_.refs_2_ = f32[7,7,8,128]{3,2,1,0:T(8,128)S(1)} collective-permute-done((f32[7,7,8,128]{3,2,1,0:T(8,128)S(1)}, f32[7,7,8,128]{3,2,1,0:T(8,128)S(1)}, u32[]{:S(2)}, u32[]{:S(2)}) %collective-permute-start.4) | collective-permute-done | bytes 200736 | tf_op jit(solution)/shard_map/ppermute | solution.py:30
  16.2 0.0 copy-done.1
  16.2 0.0 copy-start
  16.2 0.7 %copy-done = f32[7,7,8,128]{3,2,1,0:T(8,128)} copy-done((f32[7,7,8,128]{3,2,1,0:T(8,128)}, f32[7,7,8,128]{3,2,1,0:T(8,128)S(1)}, u32[]{:S(2)}) %copy-start) | copy-done | bytes 200728
  16.9 15.1 %density.1.refs_3_ = f32[25,2,128]{2,1,0:T(2,128)} custom-call(f32[7,7,8,128]{3,2,1,0:T(8,128)} %copy-done.1, f32[7,7,8,128]{3,2,1,0:T(8,128)} %copy-done, f32[7,7,8,128]{3,2,1,0:T(8,128)} %copy-done), custom_call_target="tpu_custom_call" | custom-call | tf_op jit(solution)/shard_map/density/pallas_call | solution.py:312
  32.0 0.1 collective-permute-start.5
  32.2 1.3 %collective-permute-done.5.refs_4_.refs_5_ = f32[25,2,128]{2,1,0:T(2,128)S(1)} collective-permute-done((f32[25,2,128]{2,1,0:T(2,128)}, f32[25,2,128]{2,1,0:T(2,128)S(1)}, u32[]{:S(2)}, u32[]{:S(2)}) %collective-permute-start.5) | collective-permute-done | bytes 25632 | tf_op jit(solution)/shard_map/ppermute | solution.py:30
  33.5 0.0 copy-start.2
  33.5 0.6 %copy-done.2 = f32[25,2,128]{2,1,0:T(2,128)} copy-done((f32[25,2,128]{2,1,0:T(2,128)}, f32[25,2,128]{2,1,0:T(2,128)S(1)}, u32[]{:S(2)}) %copy-start.2) | copy-done | bytes 25624
  34.1 12.1 %force.1 = f32[3,3,8,128]{3,2,1,0:T(8,128)} custom-call(f32[7,7,8,128]{3,2,1,0:T(8,128)} %copy-done.1, f32[7,7,8,128]{3,2,1,0:T(8,128)} %copy-done, f32[7,7,8,128]{3,2,1,0:T(8,128)} %copy-done, f32[25,2,128]{2,1,0:T(2,128)} %density.1.refs_3_, f32[25,2,128]{2,1,0:T(2,128)} %copy-done.2, f32[25,2,128]{2,1,0:T(2,128)} %copy-done.2), custom_call_target="tpu_custom_call" | custom-call | tf_op jit(solution)/shard_map/force/pallas_call | solution.py:324
  (7 shorter events, 0.1 us)
Async XLA Ops:
  0.0 0.8 %copy-start.3 = (s32[3,3,8,32]{3,2,1,0:T(8,128)S(1)}, s32[3,3,8,32]{3,2,1,0:T(8,128)}, u32[]{:S(2)}) copy-start(s32[3,3,8,32]{3,2,1,0:T(8,128)} %param.3) | copy-start | bytes 27652
  1.2 5.8 %collective-permute-start = (f32[2,3,8,128]{3,2,1,0:T(8,128)S(1)}, f32[2,3,8,128]{3,2,1,0:T(8,128)S(1)}, u32[]{:S(2)}, u32[]{:S(2)}) collective-permute-start(f32[2,3,8,128]{3,2,1,0:T(8,128)S(1)} %slice.19), channel_id=1, source_target_pairs={{0,8},{8,16},{16,24},{24,0},{1,9},{9,17},{17,25},{25,1},{2,10},{10... | collective-permute-start | bytes 73736 | tf_op jit(solution)/shard_map/ppermute | solution.py:30
  4.4 3.9 %collective-permute-start.1 = (f32[2,3,8,128]{3,2,1,0:T(8,128)S(1)}, f32[2,3,8,128]{3,2,1,0:T(8,128)S(1)}, u32[]{:S(2)}, u32[]{:S(2)}) collective-permute-start(f32[2,3,8,128]{3,2,1,0:T(8,128)S(1)} %slice.21), channel_id=1, source_target_pairs={{0,24},{8,0},{16,8},{24,16},{1,25},{9,1},{17,9},{25,17},{2,26},{10... | collective-permute-start | bytes 73736 | tf_op jit(solution)/shard_map/ppermute | solution.py:30
  8.3 6.1 %collective-permute-start.2 = (f32[7,2,8,128]{3,2,1,0:T(8,128)S(1)}, f32[7,2,8,128]{3,2,1,0:T(8,128)S(1)}, u32[]{:S(2)}, u32[]{:S(2)}) collective-permute-start(f32[7,2,8,128]{3,2,1,0:T(8,128)S(1)} %get-tuple-element.7), channel_id=1, source_target_pairs={{0,2},{2,4},{4,6},{6,0},{1,3},{3,5},{5,7},{7,1},{8,10},{10,12},{12... | collective-permute-start | bytes 172040 | tf_op jit(solution)/shard_map/ppermute | solution.py:30
  9.9 4.8 %collective-permute-start.3 = (f32[7,2,8,128]{3,2,1,0:T(8,128)S(1)}, f32[7,2,8,128]{3,2,1,0:T(8,128)S(1)}, u32[]{:S(2)}, u32[]{:S(2)}) collective-permute-start(f32[7,2,8,128]{3,2,1,0:T(8,128)S(1)} %get-tuple-element.8), channel_id=1, source_target_pairs={{0,6},{2,0},{4,2},{6,4},{1,7},{3,1},{5,3},{7,5},{8,14},{10,8},{12,... | collective-permute-start | bytes 172040 | tf_op jit(solution)/shard_map/ppermute | solution.py:30
  14.7 1.5 %copy-start.1 = (f32[7,7,8,128]{3,2,1,0:T(8,128)}, f32[7,7,8,128]{3,2,1,0:T(8,128)S(1)}, u32[]{:S(2)}) copy-start(f32[7,7,8,128]{3,2,1,0:T(8,128)S(1)} %pad_maximum_fusion.refs_0_) | copy-start | bytes 602116
  14.7 1.5 %collective-permute-start.4 = (f32[7,7,8,128]{3,2,1,0:T(8,128)S(1)}, f32[7,7,8,128]{3,2,1,0:T(8,128)S(1)}, u32[]{:S(2)}, u32[]{:S(2)}) collective-permute-start(f32[7,7,8,128]{3,2,1,0:T(8,128)S(1)} %pad_maximum_fusion.refs_0_), channel_id=1, source_target_pairs={{0,1},{1,0},{2,3},{3,2},{4,5},{5,4},{6,7},{7,6},{8,9},{9,8},{10,11... | collective-permute-start | bytes 602120 | tf_op jit(solution)/shard_map/ppermute | solution.py:30
  16.2 0.7 %copy-start = (f32[7,7,8,128]{3,2,1,0:T(8,128)}, f32[7,7,8,128]{3,2,1,0:T(8,128)S(1)}, u32[]{:S(2)}) copy-start(f32[7,7,8,128]{3,2,1,0:T(8,128)S(1)} %collective-permute-done.4.refs_1_.refs_2_) | copy-start | bytes 602116
  32.0 1.4 %collective-permute-start.5 = (f32[25,2,128]{2,1,0:T(2,128)}, f32[25,2,128]{2,1,0:T(2,128)S(1)}, u32[]{:S(2)}, u32[]{:S(2)}) collective-permute-start(f32[25,2,128]{2,1,0:T(2,128)} %density.1.refs_3_), channel_id=1, source_target_pairs={{0,1},{1,0},{2,3},{3,2},{4,5},{5,4},{6,7},{7,6},{8,9},{9,8},{10,11... | collective-permute-start | bytes 76808 | tf_op jit(solution)/shard_map/ppermute | solution.py:30
  33.5 0.6 %copy-start.2 = (f32[25,2,128]{2,1,0:T(2,128)}, f32[25,2,128]{2,1,0:T(2,128)S(1)}, u32[]{:S(2)}) copy-start(f32[25,2,128]{2,1,0:T(2,128)S(1)} %collective-permute-done.5.refs_4_.refs_5_) | copy-start | bytes 76804

commit v4 on v3

--- a/solution.py
+++ b/solution.py
@@ -297,6 +297,11 @@
     lax.fori_loop(0, size_x, finish, 0)
 
 
+def in_vmem(*values):
+    kept = [pltpu.with_memory_space_constraint(value, pltpu.VMEM) for value in values]
+    return kept, [pl.BlockSpec(memory_space=pltpu.VMEM) for _ in values]
+
+
 def body(positions, types):
     size_x, size_y, cells_z, slots = types.shape
     group = lanes // cells_z
@@ -309,9 +314,12 @@
     below, above = z_peers(value)
     columns = (size_x + 2) * (size_y + 2)
     f32 = jnp.float32
+    operands, specs = in_vmem(value, below, above)
     root_rows = pl.pallas_call(
         lambda *refs: density_kernel(*refs, slots=slots, group=group),
-        out_shape=jax.ShapeDtypeStruct((columns, parts, lanes), f32),
+        out_shape=pltpu.VMEM((columns, parts, lanes), f32),
+        in_specs=specs,
+        out_specs=pl.BlockSpec(memory_space=pltpu.VMEM),
         scratch_shapes=[
             pltpu.VMEM(((size_x + 4) * (size_y + 4) * 3, 4 * parts, lanes), f32),
             pltpu.VMEM(((size_x + 4) * (size_y + 4) * 3, parts, lanes), f32),
@@ -319,11 +327,13 @@
             pltpu.VMEM((columns, slots, lanes), f32),
         ],
         name="density",
-    )(value, below, above)
+    )(*operands)
     root_below, root_above = z_peers(root_rows)
+    operands, specs = in_vmem(value, below, above, root_rows, root_below, root_above)
     return pl.pallas_call(
         lambda *refs: force_kernel(*refs, slots=slots, group=group),
         out_shape=jax.ShapeDtypeStruct((size_x, size_y, cells_z, 4 * slots), f32),
+        in_specs=specs,
         scratch_shapes=[
             pltpu.VMEM((columns * 3, 4 * parts, lanes), f32),
             pltpu.VMEM((columns * 3, parts, lanes), f32),
@@ -331,7 +341,7 @@
             pltpu.VMEM((size_x * size_y, 4 * slots, lanes), f32),
         ],
         name="force",
-    )(value, below, above, root_rows, root_below, root_above)
+    )(*operands)
 
 
 def solution(mesh):

time: 46.4 us -> 42 us (0.905)
  Pallas kernels: 27.2 us -> 24.4 us
  local copies, waits for them, and re-layouts: 1.88 us -> 0.6 us
    pallas_call x1, Pallas kernels: 15.1 us -> 13.4 us  [body(): pl.pallas_call(lambda *refs: density_kernel(*refs, slots=slots, group=gro...]
    unnamed x10 -> x4, local copies, waits for them, and re-layouts: 1.3 us -> 0.01 us
    pallas_call x1, Pallas kernels: 12.1 us -> 11 us  [body(): pl.pallas_call(lambda *refs: force_kernel(*refs, slots=slots, group=group...]
where the time goes in v4:
time: 42 us; the launch traced here: 41.9 us
  Pallas kernels  24.4 us (58%)
  starting transfers between devices  8.2 us (20%)
  waiting for transfers between devices  7.73 us (18%)
  other arithmetic  0.88 us (2%)
  local copies, waits for them, and re-layouts  0.6 us (1%)
    pallas_call x1, Pallas kernels, body(): pl.pallas_call(lambda *refs: density_kernel(*refs, slots=slots, group=gro...  13.4 us
    pallas_call x1, Pallas kernels, body(): pl.pallas_call(lambda *refs: force_kernel(*refs, slots=slots, group=group...  11 us
    ppermute x6, starting transfers between devices, shifted(): lax.ppermute(value, axis, [(i, (i + step) % peers) for i in range(peers)])  8.2 us
    ppermute x6, waiting for transfers between devices, shifted(): lax.ppermute(value, axis, [(i, (i + step) % peers) for i in range(peers)])  7.73 us
  transfers between devices with their start and end apart: 6, of which 6 were waited for; matrix products, arithmetic and copies ran while one was open for 1% of the time, Pallas kernels for 0%

profile of v4, /device:TPU:0, one launch (start us, length us, event | category | flops | bytes accessed | tf_op | source)
XLA Modules:
  0.0 41.9 jit_solution(13578449736779894582)
XLA Ops:
  0.0 0.0 copy-start
  0.0 0.8 %broadcast_multiply_fusion = f32[3,3,8,96]{3,2,1,0:T(8,128)S(1)} fusion(f32[3,3,8,96]{3,2,1,0:T(8,128)} %param.2), kind=kLoop, calls=%fused_computation.4 | loop fusion | flops 6912 | bytes 55296 | tf_op jit(solution)/shard_map/mul | solution.py:310
  0.8 0.0 copy-done
  0.8 0.1 pad_maximum_fusion.1
  0.9 0.1 reshape.8
  1.0 0.1 copy.5
  1.1 0.1 slice.19
  1.2 3.0 %collective-permute-start = (f32[2,3,8,128]{3,2,1,0:T(8,128)S(1)}, f32[2,3,8,128]{3,2,1,0:T(8,128)S(1)}, u32[]{:S(2)}, u32[]{:S(2)}) collective-permute-start(f32[2,3,8,128]{3,2,1,0:T(8,128)S(1)} %slice.19), channel_id=1, source_target_pairs={{0,8},{8,16},{16,24},{24,0},{1,9},{9,17},{17,25},{25,1},{2,10},{10... | collective-permute-start | bytes 73736 | tf_op jit(solution)/shard_map/ppermute | solution.py:30
  4.3 0.1 slice.21
  4.4 1.0 %collective-permute-start.1 = (f32[2,3,8,128]{3,2,1,0:T(8,128)S(1)}, f32[2,3,8,128]{3,2,1,0:T(8,128)S(1)}, u32[]{:S(2)}, u32[]{:S(2)}) collective-permute-start(f32[2,3,8,128]{3,2,1,0:T(8,128)S(1)} %slice.21), channel_id=1, source_target_pairs={{0,24},{8,0},{16,8},{24,16},{1,25},{9,1},{17,9},{25,17},{2,26},{10... | collective-permute-start | bytes 73736 | tf_op jit(solution)/shard_map/ppermute | solution.py:30
  5.4 0.1 reshape.9
  5.5 1.5 %collective-permute-done = f32[2,3,8,128]{3,2,1,0:T(8,128)S(1)} collective-permute-done((f32[2,3,8,128]{3,2,1,0:T(8,128)S(1)}, f32[2,3,8,128]{3,2,1,0:T(8,128)S(1)}, u32[]{:S(2)}, u32[]{:S(2)}) %collective-permute-start) | collective-permute-done | bytes 24608 | tf_op jit(solution)/shard_map/ppermute | solution.py:30
  7.0 1.2 %collective-permute-done.1 = f32[2,3,8,128]{3,2,1,0:T(8,128)S(1)} collective-permute-done((f32[2,3,8,128]{3,2,1,0:T(8,128)S(1)}, f32[2,3,8,128]{3,2,1,0:T(8,128)S(1)}, u32[]{:S(2)}, u32[]{:S(2)}) %collective-permute-start.1) | collective-permute-done | bytes 24608 | tf_op jit(solution)/shard_map/ppermute | solution.py:30
  8.3 1.6 %collective-permute-start.2 = (f32[7,2,8,128]{3,2,1,0:T(8,128)S(1)}, f32[7,2,8,128]{3,2,1,0:T(8,128)S(1)}, u32[]{:S(2)}, u32[]{:S(2)}) collective-permute-start(f32[7,2,8,128]{3,2,1,0:T(8,128)S(1)} %get-tuple-element.7), channel_id=1, source_target_pairs={{0,2},{2,4},{4,6},{6,0},{1,3},{3,5},{5,7},{7,1},{8,10},{10,12},{12... | collective-permute-start | bytes 172040 | tf_op jit(solution)/shard_map/ppermute | solution.py:30
  9.9 2.2 %collective-permute-start.3 = (f32[7,2,8,128]{3,2,1,0:T(8,128)S(1)}, f32[7,2,8,128]{3,2,1,0:T(8,128)S(1)}, u32[]{:S(2)}, u32[]{:S(2)}) collective-permute-start(f32[7,2,8,128]{3,2,1,0:T(8,128)S(1)} %get-tuple-element.8), channel_id=1, source_target_pairs={{0,6},{2,0},{4,2},{6,4},{1,7},{3,1},{5,3},{7,5},{8,14},{10,8},{12,... | collective-permute-start | bytes 172040 | tf_op jit(solution)/shard_map/ppermute | solution.py:30
  12.2 2.3 %collective-permute-done.2 = f32[7,2,8,128]{3,2,1,0:T(8,128)S(1)} collective-permute-done((f32[7,2,8,128]{3,2,1,0:T(8,128)S(1)}, f32[7,2,8,128]{3,2,1,0:T(8,128)S(1)}, u32[]{:S(2)}, u32[]{:S(2)}) %collective-permute-start.2) | collective-permute-done | bytes 57376 | tf_op jit(solution)/shard_map/ppermute | solution.py:30
  14.4 0.3 collective-permute-done.3
  14.7 0.1 collective-permute-start.4
  14.8 1.4 %collective-permute-done.4.refs_1_.refs_2_ = f32[7,7,8,128]{3,2,1,0:T(8,128)S(1)} collective-permute-done((f32[7,7,8,128]{3,2,1,0:T(8,128)S(1)}, f32[7,7,8,128]{3,2,1,0:T(8,128)S(1)}, u32[]{:S(2)}, u32[]{:S(2)}) %collective-permute-start.4) | collective-permute-done | bytes 200736 | tf_op jit(solution)/shard_map/ppermute | solution.py:30
  16.2 13.4 %density.1.refs_3_ = f32[25,2,128]{2,1,0:T(2,128)S(1)} custom-call(f32[7,7,8,128]{3,2,1,0:T(8,128)S(1)} %pad_maximum_fusion.refs_0_, f32[7,7,8,128]{3,2,1,0:T(8,128)S(1)} %collective-permute-done.4.refs_1_.refs_2_, f32[7,7,8,128]{3,2,1,0:T(8,128)S(1)} %collective-permute-done.4.refs_1_.refs_2_), custom_call_target="tpu_custom_call" | custom-call | tf_op jit(solution)/shard_map/density/pallas_call | solution.py:318
  29.6 0.2 collective-permute-start.5
  29.8 1.0 %collective-permute-done.5.refs_4_.refs_5_ = f32[25,2,128]{2,1,0:T(2,128)S(1)} collective-permute-done((f32[25,2,128]{2,1,0:T(2,128)S(1)}, f32[25,2,128]{2,1,0:T(2,128)S(1)}, u32[]{:S(2)}, u32[]{:S(2)}) %collective-permute-start.5) | collective-permute-done | bytes 25632 | tf_op jit(solution)/shard_map/ppermute | solution.py:30
  30.9 11.0 %force.1 = f32[3,3,8,128]{3,2,1,0:T(8,128)} custom-call(f32[7,7,8,128]{3,2,1,0:T(8,128)S(1)} %pad_maximum_fusion.refs_0_, f32[7,7,8,128]{3,2,1,0:T(8,128)S(1)} %collective-permute-done.4.refs_1_.refs_2_, f32[7,7,8,128]{3,2,1,0:T(8,128)S(1)} %collective-permute-done.4.refs_1_.refs_2_, f32[25,2,128]{2,1,0:T(2,128)S(1)} %density.1.refs_3_, ...), custom_call_target="tpu_custom_call" | custom-call | tf_op jit(solution)/shard_map/force/pallas_call | solution.py:333
  (7 shorter events, 0.1 us)
Async XLA Ops:
  0.0 0.8 %copy-start = (s32[3,3,8,32]{3,2,1,0:T(8,128)S(1)}, s32[3,3,8,32]{3,2,1,0:T(8,128)}, u32[]{:S(2)}) copy-start(s32[3,3,8,32]{3,2,1,0:T(8,128)} %param.3) | copy-start | bytes 27652
  1.2 5.8 %collective-permute-start = (f32[2,3,8,128]{3,2,1,0:T(8,128)S(1)}, f32[2,3,8,128]{3,2,1,0:T(8,128)S(1)}, u32[]{:S(2)}, u32[]{:S(2)}) collective-permute-start(f32[2,3,8,128]{3,2,1,0:T(8,128)S(1)} %slice.19), channel_id=1, source_target_pairs={{0,8},{8,16},{16,24},{24,0},{1,9},{9,17},{17,25},{25,1},{2,10},{10... | collective-permute-start | bytes 73736 | tf_op jit(solution)/shard_map/ppermute | solution.py:30
  4.4 3.9 %collective-permute-start.1 = (f32[2,3,8,128]{3,2,1,0:T(8,128)S(1)}, f32[2,3,8,128]{3,2,1,0:T(8,128)S(1)}, u32[]{:S(2)}, u32[]{:S(2)}) collective-permute-start(f32[2,3,8,128]{3,2,1,0:T(8,128)S(1)} %slice.21), channel_id=1, source_target_pairs={{0,24},{8,0},{16,8},{24,16},{1,25},{9,1},{17,9},{25,17},{2,26},{10... | collective-permute-start | bytes 73736 | tf_op jit(solution)/shard_map/ppermute | solution.py:30
  8.3 6.1 %collective-permute-start.2 = (f32[7,2,8,128]{3,2,1,0:T(8,128)S(1)}, f32[7,2,8,128]{3,2,1,0:T(8,128)S(1)}, u32[]{:S(2)}, u32[]{:S(2)}) collective-permute-start(f32[7,2,8,128]{3,2,1,0:T(8,128)S(1)} %get-tuple-element.7), channel_id=1, source_target_pairs={{0,2},{2,4},{4,6},{6,0},{1,3},{3,5},{5,7},{7,1},{8,10},{10,12},{12... | collective-permute-start | bytes 172040 | tf_op jit(solution)/shard_map/ppermute | solution.py:30
  9.9 4.8 %collective-permute-start.3 = (f32[7,2,8,128]{3,2,1,0:T(8,128)S(1)}, f32[7,2,8,128]{3,2,1,0:T(8,128)S(1)}, u32[]{:S(2)}, u32[]{:S(2)}) collective-permute-start(f32[7,2,8,128]{3,2,1,0:T(8,128)S(1)} %get-tuple-element.8), channel_id=1, source_target_pairs={{0,6},{2,0},{4,2},{6,4},{1,7},{3,1},{5,3},{7,5},{8,14},{10,8},{12,... | collective-permute-start | bytes 172040 | tf_op jit(solution)/shard_map/ppermute | solution.py:30
  14.7 1.5 %collective-permute-start.4 = (f32[7,7,8,128]{3,2,1,0:T(8,128)S(1)}, f32[7,7,8,128]{3,2,1,0:T(8,128)S(1)}, u32[]{:S(2)}, u32[]{:S(2)}) collective-permute-start(f32[7,7,8,128]{3,2,1,0:T(8,128)S(1)} %pad_maximum_fusion.refs_0_), channel_id=1, source_target_pairs={{0,1},{1,0},{2,3},{3,2},{4,5},{5,4},{6,7},{7,6},{8,9},{9,8},{10,11... | collective-permute-start | bytes 602120 | tf_op jit(solution)/shard_map/ppermute | solution.py:30
  29.6 1.3 %collective-permute-start.5 = (f32[25,2,128]{2,1,0:T(2,128)S(1)}, f32[25,2,128]{2,1,0:T(2,128)S(1)}, u32[]{:S(2)}, u32[]{:S(2)}) collective-permute-start(f32[25,2,128]{2,1,0:T(2,128)S(1)} %density.1.refs_3_), channel_id=1, source_target_pairs={{0,1},{1,0},{2,3},{3,2},{4,5},{5,4},{6,7},{7,6},{8,9},{9,8},{10,11... | collective-permute-start | bytes 76808 | tf_op jit(solution)/shard_map/ppermute | solution.py:30
